TPU v7x, 128 devices: a whole 4x4x4 slice. The times are simulated.
128 devices in a mesh: lat: 16 (over y, x), lev: 8 (over z, core).
Axes of the slice: x: 4, y: 4, z: 4, core: 2. Of those that a mesh axis runs over, the one named last changes fastest.
Arguments:
- activations: bfloat16 [176, 819200], P(None, ('lat', 'lev')), may hold values from -6 to 6
- out_cotangent: bfloat16 [176, 819200], P(None, ('lat', 'lev')), may hold values from -6 to 6
- weight_in: bfloat16 [176, 384], replicated, may hold values from -0.4375 to 0.4375
- weight_mid: bfloat16 [384, 384], replicated, may hold values from -0.3125 to 0.3125
- weight_out: bfloat16 [176, 384], replicated, may hold values from -0.3125 to 0.3125
- legendre: bfloat16 [640, 320, 640], P(('lat', 'lev')), may hold values from -0.25 to 0.25
- level_inverse: bfloat16 [88, 88, 640], replicated, may hold values from -0.625 to 0.625
- wave_order: int32 [640], replicated, may hold values from 0 to 639, each once
Outputs:
- grad_input: float32 [176, 384], replicated
- grad_middle: float32 [384, 384], replicated
- grad_output: float32 [176, 384], replicated
- grid_cotangent: float32 [176, 640, 1280], P(None, ('lat', 'lev'))
Inputs may be any that keep to these rules, and one draw needn't show every extreme that they name: wave_order is a permutation of 0 to 639; the device at index d of lat and lev taken together (lat major) holds the d-th block of slots of legendre.
All inputs are finite; a program needn't handle non-finite values.
Results may differ from a plain program's by a relative error of at most 0.017.
Values may be sent and summed in bfloat16 or wider, within the bound.
No kernel may reach another device: no remote copies, remote signals or barrier semaphores. Data moves between devices by JAX's collectives and lax.ppermute only.
A program may use at most 192 MiB of HBM per device.

v0:
```python
import math
from functools import partial

import jax
import jax.numpy as jnp
from jax import lax
from jax.experimental import pallas as pl
from jax.experimental.pallas import tpu as pltpu
from jax.sharding import PartitionSpec as P

NLAT = 640
NLON = 1280
LEVELS = 88
FEATURES = 176
HIDDEN = 384
NDEG = 640
HALF = NLAT // 2
SLOTS = 5
WAYS = 128
LONB = 160
LANES = 128
WIDTH = 896
TILES = WIDTH // LANES
DATA_ROWS = 2 * SLOTS * TILES
GRAD_ROWS = 18
ROWS = DATA_ROWS + GRAD_ROWS
COLS = 6400
TILE = 256
STEPS = COLS // TILE
BANK = 24
EVERYWHERE = ("lat", "lev")

VMEM = pl.BlockSpec(memory_space=pltpu.VMEM)
SMEM = pl.BlockSpec(memory_space=pltpu.SMEM)
ANY = pl.BlockSpec(memory_space=pl.ANY)


def mm(left, right):
    return jnp.dot(left, right, preferred_element_type=jnp.float32)


def mm_nt(left, right):
    return lax.dot_general(left, right, (((1,), (1,)), ((), ())), preferred_element_type=jnp.float32)


def mm_tn(left, right):
    return lax.dot_general(left, right, (((0,), (0,)), ((), ())), preferred_element_type=jnp.float32)


def params(mib):
    return pltpu.CompilerParams(vmem_limit_bytes=mib * 1024 * 1024)


def column_kernel(x_ref, c_ref, wi_ref, wm_ref, wo_ref, out_ref, grad_ref, wit, wmt, wot, grid_ref, g1, g2, g3):
    n = pl.program_id(0)

    @pl.when(n == 0)
    def _():
        wit[...] = wi_ref[...].T
        wmt[...] = wm_ref[...].T
        wot[...] = wo_ref[...].T
        g1[...] = jnp.zeros_like(g1)
        g2[...] = jnp.zeros_like(g2)
        g3[...] = jnp.zeros_like(g3)
        grid_ref[SLOTS * FEATURES :, :] = jnp.zeros((WIDTH - SLOTS * FEATURES, NLON), jnp.bfloat16)

    x = x_ref[...]
    c = c_ref[...]
    pre1 = mm(wit[...], x)
    s1 = 0.5 * jnp.tanh(0.5 * pre1) + 0.5
    silu1 = pre1 * s1
    slope1 = s1 + silu1 * (1.0 - s1)
    h1 = silu1.astype(jnp.bfloat16)
    pre2 = mm(wmt[...], h1)
    s2 = 0.5 * jnp.tanh(0.5 * pre2) + 0.5
    silu2 = pre2 * s2
    slope2 = s2 + silu2 * (1.0 - s2)
    h2 = silu2.astype(jnp.bfloat16)
    d2 = (mm(wot[...], c) * slope2).astype(jnp.bfloat16)
    d1 = (mm(wm_ref[...], d2) * slope1).astype(jnp.bfloat16)
    gi = mm(wi_ref[...], d1).astype(jnp.bfloat16)
    g1[...] += mm_nt(x, d1)
    g2[...] += mm_nt(h1, d2)
    g3[...] += mm_nt(c, h2)
    band = n // (NLON // TILE)
    part = n % (NLON // TILE)
    grid_ref[pl.ds(pl.multiple_of(band * FEATURES, 16), FEATURES), pl.ds(pl.multiple_of(part * TILE, TILE), TILE)] = gi

    @pl.when(n == STEPS - 1)
    def _():
        for t in range(TILES):
            out_ref[:, LANES * t : LANES * (t + 1)] = grid_ref[LANES * t : LANES * (t + 1), :].T
        at = 0
        for g in (g1, g2, g3):
            rows = g.shape[0]
            for t in range(HIDDEN // LANES):
                grad_ref[at : at + rows, :] = g[:, LANES * t : LANES * (t + 1)]
                at += rows
        grad_ref[at:, :] = jnp.zeros((GRAD_ROWS * WAYS - at, LANES), jnp.float32)


def columns(x, c, wi, wm, wo):
    block = pl.BlockSpec((FEATURES, TILE), lambda n: (0, n))
    return pl.pallas_call(
        column_kernel,
        grid=(STEPS,),
        in_specs=[block, block] + [pl.BlockSpec(w.shape, lambda n: (0, 0)) for w in (wi, wm, wo)],
        out_specs=[
            pl.BlockSpec((NLON, WIDTH), lambda n: (0, 0)),
            pl.BlockSpec((GRAD_ROWS * WAYS, LANES), lambda n: (0, 0)),
        ],
        out_shape=[
            jax.ShapeDtypeStruct((NLON, WIDTH), jnp.bfloat16),
            jax.ShapeDtypeStruct((GRAD_ROWS * WAYS, LANES), jnp.float32),
        ],
        scratch_shapes=[
            pltpu.VMEM((HIDDEN, FEATURES), jnp.bfloat16),
            pltpu.VMEM((HIDDEN, HIDDEN), jnp.bfloat16),
            pltpu.VMEM((HIDDEN, FEATURES), jnp.bfloat16),
            pltpu.VMEM((WIDTH, NLON), jnp.bfloat16),
            pltpu.VMEM((FEATURES, HIDDEN), jnp.float32),
            pltpu.VMEM((HIDDEN, HIDDEN), jnp.float32),
            pltpu.VMEM((FEATURES, HIDDEN), jnp.float32),
        ],
        compiler_params=params(48),
        name="columns",
    )(x, c, wi, wm, wo)


def wave_kernel(ca_ref, sa_ref, cb_ref, sb_ref, out_ref):
    for s in range(SLOTS):
        rows = slice(WAYS * s, WAYS * (s + 1))
        cb, sb = cb_ref[rows, :], sb_ref[rows, :]
        for a in range(NLON // LANES):
            ca, sa = ca_ref[rows, a : a + 1], sa_ref[rows, a : a + 1]
            cols = slice(LANES * a, LANES * (a + 1))
            out_ref[WAYS * 2 * s : WAYS * (2 * s + 1), cols] = (ca * cb - sa * sb).astype(jnp.bfloat16)
            out_ref[WAYS * (2 * s + 1) : WAYS * (2 * s + 2), cols] = (-(sa * cb + ca * sb)).astype(jnp.bfloat16)


def wave_table(wave_order):
    m = wave_order.reshape(WAYS, SLOTS).T.reshape(NLAT, 1)
    turn = 2.0 * math.pi / NLON
    fine = (m * jnp.arange(LANES, dtype=jnp.int32)[None, :] % NLON).astype(jnp.float32) * turn
    coarse = (m * (LANES * jnp.arange(NLON // LANES, dtype=jnp.int32))[None, :] % NLON).astype(jnp.float32) * turn
    scale = 1.0 / math.sqrt(NLON)
    return pl.pallas_call(
        wave_kernel,
        in_specs=[VMEM] * 4,
        out_specs=VMEM,
        out_shape=jax.ShapeDtypeStruct((NLON, NLON), jnp.bfloat16),
        compiler_params=params(32),
        name="waves",
    )(jnp.cos(coarse), jnp.sin(coarse), jnp.cos(fine) * scale, jnp.sin(fine) * scale)


def legendre_kernel(m_ref, leg_ref, at_ref, as_ref):
    m = m_ref[pl.program_id(0)]
    leg = leg_ref[0]
    row = lax.broadcasted_iota(jnp.int32, (HALF, NLAT), 0)
    col = lax.broadcasted_iota(jnp.int32, (HALF, NLAT), 1)
    lat = 40 * ((col & 127) >> 3) + 8 * (col >> 7) + (col & 7)
    pick = (jnp.where(lat < HALF, lat, NLAT - 1 - lat) == row).astype(jnp.bfloat16)
    full = mm_tn(leg, pick)
    deg = lax.broadcasted_iota(jnp.int32, (NDEG, NLAT), 0)
    col = lax.broadcasted_iota(jnp.int32, (NDEG, NLAT), 1)
    south = (col & 127) >= 64
    full = jnp.where(south & (((deg + m) & 1) == 1), -full, full)
    at_ref[0] = jnp.where(deg >= m, full, 0.0).astype(jnp.bfloat16)
    row = lax.broadcasted_iota(jnp.int32, (NLAT, HALF), 0)
    col = lax.broadcasted_iota(jnp.int32, (NLAT, HALF), 1)
    lat = 5 * (row & 127) + (row >> 7)
    pick = (jnp.where(lat < HALF, lat, NLAT - 1 - lat) == col).astype(jnp.bfloat16)
    full = mm(pick, leg)
    row = lax.broadcasted_iota(jnp.int32, (NLAT, NDEG), 0)
    deg = lax.broadcasted_iota(jnp.int32, (NLAT, NDEG), 1)
    south = (row & 127) >= 64
    full = jnp.where(south & (((deg + m) & 1) == 1), -full, full)
    as_ref[0] = jnp.where(deg >= m, full, 0.0).astype(jnp.bfloat16)


def legendre_tables(wave_local, legendre):
    block = pl.BlockSpec((1, NDEG, NLAT), lambda s, m: (s, 0, 0))
    table = jax.ShapeDtypeStruct((SLOTS, NDEG, NLAT), jnp.bfloat16)
    return pl.pallas_call(
        legendre_kernel,
        grid_spec=pltpu.PrefetchScalarGridSpec(
            num_scalar_prefetch=1,
            grid=(SLOTS,),
            in_specs=[pl.BlockSpec((1, HALF, NDEG), lambda s, m: (s, 0, 0))],
            out_specs=[block, block],
        ),
        out_shape=[table, table],
        compiler_params=params(40),
        name="legendre",
    )(wave_local, legendre)


def pack_out(wide_ref, out_ref):
    def body(p, carry):
        out_ref[p] = wide_ref[pl.ds(pl.multiple_of(ROWS * p, 8), ROWS), :].astype(jnp.bfloat16)
        return carry

    lax.fori_loop(0, WAYS, body, 0, unroll=4)


def unpack_in(in_ref, wide_ref):
    def body(p, carry):
        wide_ref[pl.ds(pl.multiple_of(ROWS * p, 8), ROWS), :] = in_ref[p].astype(jnp.float32)
        return carry

    lax.fori_loop(0, WAYS, body, 0, unroll=4)


def forward_kernel(x_ref, table_ref, grad_ref, out_ref, wide_ref):
    def body(k, carry):
        piece = mm(table_ref[pl.ds(pl.multiple_of(256 * k, 256), 256), :], x_ref[...])
        for h in range(2):
            for t in range(TILES):
                wide_ref[pl.ds((2 * k + h) * TILES + t, WAYS, stride=ROWS), :] = piece[
                    WAYS * h : WAYS * (h + 1), LANES * t : LANES * (t + 1)
                ]
        return carry

    lax.fori_loop(0, SLOTS, body, 0)
    for k in range(GRAD_ROWS):
        wide_ref[pl.ds(DATA_ROWS + k, WAYS, stride=ROWS), :] = grad_ref[WAYS * k : WAYS * (k + 1), :]
    pack_out(wide_ref, out_ref)


def forward(x, table, grad):
    return pl.pallas_call(
        forward_kernel,
        in_specs=[VMEM] * 3,
        out_specs=VMEM,
        out_shape=jax.ShapeDtypeStruct((WAYS, ROWS, LANES), jnp.bfloat16),
        scratch_shapes=[pltpu.VMEM((WAYS * ROWS, LANES), jnp.float32)],
        compiler_params=params(48),
        name="forward",
    )(x, table, grad)


def spectral_kernel(m_ref, in_ref, at_ref, inv_hbm, as_hbm, out_ref, wide_ref, x_ref, bank_ref, inv_ref, as_ref, sums_ref, sems):
    inv_copy = pltpu.make_async_copy(inv_hbm, inv_ref, sems.at[0])
    as_copy = pltpu.make_async_copy(as_hbm, as_ref, sems.at[1])
    inv_copy.start()
    as_copy.start()
    unpack_in(in_ref, wide_ref)
    for k in range(GRAD_ROWS):
        slab = wide_ref[pl.ds(DATA_ROWS + k, WAYS, stride=ROWS), :]
        sums_ref[k : k + 1, :] = jnp.sum(slab, axis=0, keepdims=True)
    lane = lax.broadcasted_iota(jnp.int32, (WAYS, LANES), 1)

    def analyse(s, carry):
        for r in range(2):
            tiles = [wide_ref[pl.ds((2 * s + r) * TILES + t, WAYS, stride=ROWS), :] for t in range(TILES)]
            for g in range(2 * SLOTS):
                t, off = divmod(LEVELS * g, LANES)
                piece = tiles[t]
                if off:
                    piece = pltpu.roll(piece, LANES - off, 1)
                    if off + LEVELS > LANES:
                        piece = jnp.where(lane < LANES - off, piece, pltpu.roll(tiles[t + 1], LANES - off, 1))
                i, a = divmod(g, 2)
                x_ref[WAYS * i : WAYS * (i + 1), LANES * (2 * r + a) : LANES * (2 * r + a + 1)] = piece.astype(jnp.bfloat16)
        y = mm(at_ref[s], x_ref[...])
        for j in range(4):
            bank_ref[pl.ds(4 * s + j, NDEG, stride=BANK), :] = y[:, LANES * j : LANES * (j + 1)]
        return carry

    lax.fori_loop(0, SLOTS, analyse, 0)
    inv_copy.wait()

    def solve(k, carry):
        for u in range(16):
            deg = 16 * k + u
            rows = pl.ds(pl.multiple_of(deg * BANK, 8), BANK)
            bank_ref[rows, :LEVELS] = mm(bank_ref[rows, :LEVELS].astype(jnp.bfloat16), inv_ref[deg])
        return carry

    lax.fori_loop(0, NDEG // 16, solve, 0)
    as_copy.wait()

    def synthesise(s, carry):
        z = jnp.concatenate(
            [bank_ref[pl.ds(4 * s + j, NDEG, stride=BANK), :].astype(jnp.bfloat16) for j in range(4)], axis=1
        )
        weight = jnp.where(m_ref[s] == 0, 1.0, 2.0)
        w = mm(as_ref[s], z) * weight
        for r in range(2):
            tiles = [None] * TILES
            for g in range(2 * SLOTS):
                i, a = divmod(g, 2)
                piece = w[WAYS * i : WAYS * (i + 1), LANES * (2 * r + a) : LANES * (2 * r + a + 1)]
                t, off = divmod(LEVELS * g, LANES)
                if off:
                    piece = pltpu.roll(piece, off, 1)
                tiles[t] = piece if off == 0 else jnp.where(lane < off, tiles[t], piece)
                if off + LEVELS > LANES:
                    tiles[t + 1] = piece
            for t in range(TILES):
                wide_ref[pl.ds((2 * s + r) * TILES + t, WAYS, stride=ROWS), :] = tiles[t]
        return carry

    lax.fori_loop(0, SLOTS, synthesise, 0)
    for k in range(GRAD_ROWS):
        wide_ref[pl.ds(DATA_ROWS + k, WAYS, stride=ROWS), :] = jnp.broadcast_to(sums_ref[k : k + 1, :], (WAYS, LANES))
    pack_out(wide_ref, out_ref)


def spectral(wave_local, arrived, at, inv, synth):
    return pl.pallas_call(
        spectral_kernel,
        in_specs=[SMEM, VMEM, VMEM, ANY, ANY],
        out_specs=VMEM,
        out_shape=jax.ShapeDtypeStruct((WAYS, ROWS, LANES), jnp.bfloat16),
        scratch_shapes=[
            pltpu.VMEM((WAYS * ROWS, LANES), jnp.float32),
            pltpu.VMEM((NLAT, 4 * LANES), jnp.bfloat16),
            pltpu.VMEM((NDEG * BANK, LANES), jnp.float32),
            pltpu.VMEM((NDEG, LEVELS, LEVELS), jnp.bfloat16),
            pltpu.VMEM((SLOTS, NLAT, NDEG), jnp.bfloat16),
            pltpu.VMEM((24, LANES), jnp.float32),
            pltpu.SemaphoreType.DMA((2,)),
        ],
        compiler_params=params(58),
        name="spectral",
    )(wave_local, arrived, at, inv, synth)


def inverse_kernel(in_ref, table_ref, out_ref, g1, g2, g3, wide_ref, rows_ref, grad_ref):
    unpack_in(in_ref, wide_ref)
    for t in range(TILES):
        for c in range(2 * SLOTS):
            slab = wide_ref[pl.ds(TILES * c + t, WAYS, stride=ROWS), :]
            rows_ref[LANES * t : LANES * (t + 1), WAYS * c : WAYS * (c + 1)] = slab.T.astype(jnp.bfloat16)
    for i in range(SLOTS):
        out_ref[i] = mm(rows_ref[FEATURES * i : FEATURES * (i + 1), :], table_ref[...])
    for k in range(GRAD_ROWS):
        grad_ref[WAYS * k : WAYS * (k + 1), :] = wide_ref[pl.ds(DATA_ROWS + k, WAYS, stride=ROWS), :]
    scale = 1.0 / math.sqrt(NLAT * NLON)
    at = 0
    for g in (g1, g2, g3):
        rows = g.shape[0]
        for t in range(HIDDEN // LANES):
            g[:, LANES * t : LANES * (t + 1)] = grad_ref[at : at + rows, :] * scale
            at += rows


def inverse(arrived, table):
    return pl.pallas_call(
        inverse_kernel,
        in_specs=[VMEM] * 2,
        out_specs=[VMEM] * 4,
        out_shape=[
            jax.ShapeDtypeStruct((SLOTS, FEATURES, NLON), jnp.float32),
            jax.ShapeDtypeStruct((FEATURES, HIDDEN), jnp.float32),
            jax.ShapeDtypeStruct((HIDDEN, HIDDEN), jnp.float32),
            jax.ShapeDtypeStruct((FEATURES, HIDDEN), jnp.float32),
        ],
        scratch_shapes=[
            pltpu.VMEM((WAYS * ROWS, LANES), jnp.float32),
            pltpu.VMEM((WIDTH, NLON), jnp.bfloat16),
            pltpu.VMEM((GRAD_ROWS * WAYS, LANES), jnp.float32),
        ],
        compiler_params=params(48),
        name="inverse",
    )(arrived, table)


def swap(array, axis):
    return lax.all_to_all(array, axis, split_axis=0, concat_axis=0, tiled=True)


def on_device(x, c, wi, wm, wo, legendre, level_inverse, wave_order):
    grid, grad = columns(x, c, wi, wm, wo)
    grid, legendre, level_inverse, wave_order = lax.optimization_barrier((grid, legendre, level_inverse, wave_order))
    rows = swap(grid.reshape(8, LONB, WIDTH), "lev").reshape(NLON, WIDTH)
    wave_local = lax.dynamic_slice_in_dim(wave_order, lax.axis_index(EVERYWHERE) * SLOTS, SLOTS)
    table = wave_table(wave_order)
    at, synth = legendre_tables(wave_local, legendre)
    inv = level_inverse.transpose(2, 0, 1)
    arrived = swap(forward(rows, table, grad), EVERYWHERE)
    arrived = swap(spectral(wave_local, arrived, at, inv, synth), EVERYWHERE)
    out, g1, g2, g3 = inverse(arrived, table)
    return g1, g2, g3, out.transpose(1, 0, 2)


def solution(mesh):
    in_specs = (
        P(None, EVERYWHERE),
        P(None, EVERYWHERE),
        P(),
        P(),
        P(),
        P(EVERYWHERE, None, None),
        P(),
        P(),
    )
    out_specs = (P(), P(), P(), P(None, EVERYWHERE, None))
    return jax.shard_map(on_device, mesh=mesh, in_specs=in_specs, out_specs=out_specs, check_vma=False)
```

profile of v0, /device:TPU:0, one launch (start us, length us, event | category | flops | bytes accessed | tf_op | source)
XLA Modules:
  0.0 206.7 jit_solution(3980629244791323191)
XLA Ops:
  0.6 1.6 copy-done.4
  2.3 1.0 copy-done.6
  3.2 0.9 copy-done.7
  4.1 0.9 copy-done.8
  5.0 36.2 %columns.1 = (bf16[1280,896]{1,0:T(8,128)(2,1)}, f32[2304,128]{1,0:T(8,128)S(1)}) custom-call(bf16[176,6400]{1,0:T(8,128)(2,1)S(1)} %copy-done.4, bf16[176,6400]{1,0:T(8,128)(2,1)} %c_ref.1, bf16[176,384]{1,0:T(8,128)(2,1)S(1)} %copy-done.7, bf16[384,384]{1,0:T(8,128)(2,1)S(1)} %copy-done.6, bf16[176,384]{1,0:T(8,128)(2,1)S(1)} %copy-done.8), custom_call_target="tpu_custom_call" | custom-call | tf_op jit(solution)/shard_map/columns/pallas_call | solution.py:104
  41.3 5.6 %all-to-all-start = ((bf16[8,160,896]{2,1,0:T(8,128)(2,1)}), bf16[8,160,896]{2,1,0:T(8,128)(2,1)S(1)}, u32[]{:S(2)}, u32[]{:S(2)}) async-start(bf16[8,160,896]{2,1,0:T(8,128)(2,1)} %bitcast.8), calls=%async_computation | async-start | bytes 4587520 | tf_op jit(solution)/shard_map/all_to_all | solution.py:372
  46.8 0.2 reshape.25
  47.1 0.1 fusion.5
  47.2 0.9 copy.16
  48.1 1.4 sine_multiply_fusion
  49.5 2.1 %multiply_sine_fusion = (f32[640,10]{1,0:T(8,128)S(1)}, f32[640,10]{1,0:T(8,128)S(1)}) fusion(f32[640,10]{1,0:T(8,128)} %copy.16), kind=kLoop, calls=%fused_computation.9 | loop fusion | flops 6400 | bytes 76800 | tf_op jit(solution)/shard_map/sin | solution.py:154
  51.7 1.8 waves.1.table_ref
  53.5 1.7 copy-done
  55.2 20.9 %all-to-all-done = bf16[8,160,896]{2,1,0:T(8,128)(2,1)S(1)} async-done(((bf16[8,160,896]{2,1,0:T(8,128)(2,1)}), bf16[8,160,896]{2,1,0:T(8,128)(2,1)S(1)}, u32[]{:S(2)}, u32[]{:S(2)}) %all-to-all-start) | async-done | bytes 2293792 | tf_op jit(solution)/shard_map/all_to_all | solution.py:372
  76.1 8.7 %forward.1 = bf16[128,88,128]{2,1,0:T(8,128)(2,1)} custom-call(bf16[1280,896]{1,0:T(8,128)(2,1)S(1)} %bitcast.6, bf16[1280,1280]{1,0:T(8,128)(2,1)} %copy-done, f32[2304,128]{1,0:T(8,128)S(1)} %get-tuple-element.19.grad_ref), custom_call_target="tpu_custom_call" | custom-call | tf_op jit(solution)/shard_map/forward/pallas_call | solution.py:232
  84.8 8.7 %all-to-all-start.1 = ((bf16[128,88,128]{2,1,0:T(8,128)(2,1)}), bf16[128,88,128]{2,1,0:T(8,128)(2,1)}, u32[]{:S(2)}, u32[]{:S(2)}) async-start(bf16[128,88,128]{2,1,0:T(8,128)(2,1)} %forward.1), calls=%async_computation.1 | async-start | bytes 5767168 | tf_op jit(solution)/shard_map/all_to_all | solution.py:372
  93.6 19.0 %copy.17 = bf16[88,88,640]{1,0,2:T(8,128)(2,1)} copy(bf16[88,88,640]{2,1,0:T(8,128)(2,1)} %param.14) | data formatting | bytes 19824640 | tf_op jit(solution)/shard_map/optimization_barrier | solution.py:377
  112.6 7.7 %legendre.1 = (bf16[5,640,640]{2,1,0:T(8,128)(2,1)S(1)}, bf16[5,640,640]{2,1,0:T(8,128)(2,1)S(1)}) custom-call(s32[5]{0:T(128)S(1)} %dynamic_slice.3.m_ref, bf16[5,320,640]{2,1,0:T(8,128)(2,1)S(1)} %copy-done.5), custom_call_target="tpu_custom_call" | custom-call | tf_op jit(solution)/shard_map/legendre/pallas_call | solution.py:185
  120.3 2.0 copy-done.2
  122.3 1.9 copy-done.3
  124.2 7.7 %all-to-all-done.1.in_ref = bf16[128,88,128]{2,1,0:T(8,128)(2,1)} async-done(((bf16[128,88,128]{2,1,0:T(8,128)(2,1)}), bf16[128,88,128]{2,1,0:T(8,128)(2,1)}, u32[]{:S(2)}, u32[]{:S(2)}) %all-to-all-start.1) | async-done | bytes 2883616 | tf_op jit(solution)/shard_map/all_to_all | solution.py:372
  131.9 24.5 %spectral.1 = bf16[128,88,128]{2,1,0:T(8,128)(2,1)} custom-call(s32[5]{0:T(128)} %copy-done.9, bf16[128,88,128]{2,1,0:T(8,128)(2,1)} %all-to-all-done.1.in_ref, bf16[5,640,640]{2,1,0:T(8,128)(2,1)} %copy-done.2, bf16[640,88,88]{2,1,0:T(8,128)(2,1)} %bitcast.7, bf16[5,640,640]{2,1,0:T(8,128)(2,1)} %copy-done.3), custom_call_target="tpu_custom_call" | custom-call | tf_op jit(solution)/shard_map/spectral/pallas_call | solution.py:312
  156.4 44.1 %all_to_all.15.in_ref = bf16[128,88,128]{2,1,0:T(8,128)(2,1)S(1)} all-to-all(bf16[128,88,128]{2,1,0:T(8,128)(2,1)} %spectral.1), channel_id=1, replica_groups=mesh['lat'=16,'lev'=8] {'lat','lev'}, dimensions={0} | all-to-all | bytes 5767168 | tf_op jit(solution)/shard_map/all_to_all | solution.py:372
  200.5 6.2 %inverse.1 = (f32[5,176,1280]{2,1,0:T(8,128)}, f32[176,384]{1,0:T(8,128)}, f32[384,384]{1,0:T(8,128)}, f32[176,384]{1,0:T(8,128)}) custom-call(bf16[128,88,128]{2,1,0:T(8,128)(2,1)S(1)} %all_to_all.15.in_ref, bf16[1280,1280]{1,0:T(8,128)(2,1)S(1)} %copy-done.1), custom_call_target="tpu_custom_call" | custom-call | tf_op jit(solution)/shard_map/inverse/pallas_call | solution.py:351
  (18 shorter events, 0.2 us)
Async XLA Ops:
  0.6 1.6 copy-start.4
  2.3 1.0 copy-start.6
  3.2 0.9 copy-start.7
  4.1 0.9 copy-start.8
  41.3 5.6 %copy-start.10 = (s32[640]{0:T(1024)S(1)}, s32[640]{0:T(1024)}, u32[]{:S(2)}) copy-start(s32[640]{0:T(1024)} %param.15) | copy-start | bytes 7684
  41.3 34.8 %all-to-all-start = ((bf16[8,160,896]{2,1,0:T(8,128)(2,1)}), bf16[8,160,896]{2,1,0:T(8,128)(2,1)S(1)}, u32[]{:S(2)}, u32[]{:S(2)}) async-start(bf16[8,160,896]{2,1,0:T(8,128)(2,1)} %bitcast.8), calls=%async_computation | async-start | bytes 4587520 | tf_op jit(solution)/shard_map/all_to_all | solution.py:372
  53.5 1.7 copy-start
  84.8 47.1 %all-to-all-start.1 = ((bf16[128,88,128]{2,1,0:T(8,128)(2,1)}), bf16[128,88,128]{2,1,0:T(8,128)(2,1)}, u32[]{:S(2)}, u32[]{:S(2)}) async-start(bf16[128,88,128]{2,1,0:T(8,128)(2,1)} %forward.1), calls=%async_computation.1 | async-start | bytes 5767168 | tf_op jit(solution)/shard_map/all_to_all | solution.py:372
  93.6 19.0 %copy-start.9 = (s32[5]{0:T(128)}, s32[5]{0:T(128)S(1)}, u32[]{:S(2)}) copy-start(s32[5]{0:T(128)S(1)} %dynamic_slice.3.m_ref) | copy-start | bytes 64
  93.6 19.0 %copy-start.5 = (bf16[5,320,640]{2,1,0:T(8,128)(2,1)S(1)}, bf16[5,320,640]{2,1,0:T(8,128)(2,1)}, u32[]{:S(2)}) copy-start(bf16[5,320,640]{2,1,0:T(8,128)(2,1)} %leg_ref) | copy-start | bytes 6144004
  120.3 2.0 copy-start.2
  122.3 1.9 copy-start.3
  156.4 44.1 %copy-start.1 = (bf16[1280,1280]{1,0:T(8,128)(2,1)S(1)}, bf16[1280,1280]{1,0:T(8,128)(2,1)}, u32[]{:S(2)}) copy-start(bf16[1280,1280]{1,0:T(8,128)(2,1)} %copy-done) | copy-start | bytes 9830404
where the time goes:
time: 208 us; the launch traced here: 207 us
  Pallas kernels  85.2 us (41%)
  blocking collectives  44.1 us (21%)
  local copies, waits for them, and re-layouts  30.3 us (15%)
  waiting for transfers between devices  28.6 us (14%)
  starting transfers between devices  14.2 us (7%)
  other arithmetic  3.64 us (2%)
    all_to_all x1, blocking collectives, swap(): return lax.all_to_all(array, axis, split_axis=0, concat_axis=0, tiled=True)  44.1 us
    pallas_call x1, Pallas kernels, columns(): pl.pallas_call(column_kernel, grid=(STEPS,), in_specs=[block, block] + [p...  36.2 us
    all_to_all x2, waiting for transfers between devices, swap(): return lax.all_to_all(array, axis, split_axis=0, concat_axis=0, tiled=True)  28.6 us
    pallas_call x1, Pallas kernels, spectral(): pl.pallas_call(spectral_kernel, in_specs=[SMEM, VMEM, VMEM, ANY, ANY], ou...  24.5 us
    optimization_barrier x1, local copies, waits for them, and re-layouts, on_device(): lax.optimization_barrier((grid, legendre, level_inverse, wave_order))  19 us
    all_to_all x2, starting transfers between devices, swap(): return lax.all_to_all(array, axis, split_axis=0, concat_axis=0, tiled=True)  14.2 us
    unnamed x22, local copies, waits for them, and re-layouts  10 us
    pallas_call x1, Pallas kernels, forward(): pl.pallas_call(forward_kernel, in_specs=[VMEM] * 3, out_specs=VMEM, out_s...  8.71 us
  transfers between devices with their start and end apart: 2, of which 2 were waited for; matrix products, arithmetic and copies ran while one was open for 12% of the time, Pallas kernels for 5%

commit v1 on v0

--- a/solution.py
+++ b/solution.py
@@ -26,8 +26,9 @@
 ROWS = DATA_ROWS + GRAD_ROWS
 COLS = 6400
 TILE = 256
-STEPS = COLS // TILE
-BANK = 24
+STEPS = COLS // NLON
+BANK = 25
+PITCH = 89
 EVERYWHERE = ("lat", "lev")
 
 VMEM = pl.BlockSpec(memory_space=pltpu.VMEM)
@@ -51,40 +52,47 @@
     return pltpu.CompilerParams(vmem_limit_bytes=mib * 1024 * 1024)
 
 
-def column_kernel(x_ref, c_ref, wi_ref, wm_ref, wo_ref, out_ref, grad_ref, wit, wmt, wot, grid_ref, g1, g2, g3):
+def column_kernel(x_ref, c_ref, wi_ref, wm_ref, wo_ref, out_ref, grad_ref, wit, wmt, wot, wmh, h1_ref, h2_ref, d1_ref, d2_ref, s1_ref, grid_ref, g1, g2, g3):
     n = pl.program_id(0)
 
     @pl.when(n == 0)
     def _():
-        wit[...] = wi_ref[...].T
-        wmt[...] = wm_ref[...].T
-        wot[...] = wo_ref[...].T
+        half = jnp.bfloat16(0.5)
+        wit[...] = wi_ref[...].T * half
+        wmt[...] = wm_ref[...].T * half
+        wot[...] = wo_ref[...].T * half
+        wmh[...] = wm_ref[...] * half
         g1[...] = jnp.zeros_like(g1)
         g2[...] = jnp.zeros_like(g2)
         g3[...] = jnp.zeros_like(g3)
         grid_ref[SLOTS * FEATURES :, :] = jnp.zeros((WIDTH - SLOTS * FEATURES, NLON), jnp.bfloat16)
 
-    x = x_ref[...]
-    c = c_ref[...]
-    pre1 = mm(wit[...], x)
-    s1 = 0.5 * jnp.tanh(0.5 * pre1) + 0.5
-    silu1 = pre1 * s1
-    slope1 = s1 + silu1 * (1.0 - s1)
-    h1 = silu1.astype(jnp.bfloat16)
-    pre2 = mm(wmt[...], h1)
-    s2 = 0.5 * jnp.tanh(0.5 * pre2) + 0.5
-    silu2 = pre2 * s2
-    slope2 = s2 + silu2 * (1.0 - s2)
-    h2 = silu2.astype(jnp.bfloat16)
-    d2 = (mm(wot[...], c) * slope2).astype(jnp.bfloat16)
-    d1 = (mm(wm_ref[...], d2) * slope1).astype(jnp.bfloat16)
-    gi = mm(wi_ref[...], d1).astype(jnp.bfloat16)
-    g1[...] += mm_nt(x, d1)
-    g2[...] += mm_nt(h1, d2)
-    g3[...] += mm_nt(c, h2)
-    band = n // (NLON // TILE)
-    part = n % (NLON // TILE)
-    grid_ref[pl.ds(pl.multiple_of(band * FEATURES, 16), FEATURES), pl.ds(pl.multiple_of(part * TILE, TILE), TILE)] = gi
+    band = pl.ds(pl.multiple_of(n * FEATURES, 16), FEATURES)
+    tiles = [slice(TILE * t, TILE * (t + 1)) for t in range(NLON // TILE)]
+    parts = [slice(384 * t, 384 * (t + 1)) for t in range(HIDDEN // 384)]
+    for cols in tiles:
+        for rows in parts:
+            u = mm(wit[rows, :], x_ref[:, cols])
+            tanh = jnp.tanh(u)
+            p = 1.0 + tanh
+            h1_ref[rows, cols] = (u * p).astype(jnp.bfloat16)
+            s1_ref[rows, cols] = p * (1.0 + u * (1.0 - tanh))
+    for cols in tiles:
+        for rows in parts:
+            u = mm(wmt[rows, :], h1_ref[:, cols])
+            back = mm(wot[rows, :], c_ref[:, cols])
+            tanh = jnp.tanh(u)
+            p = 1.0 + tanh
+            h2_ref[rows, cols] = (u * p).astype(jnp.bfloat16)
+            d2_ref[rows, cols] = (back * (p * (1.0 + u * (1.0 - tanh)))).astype(jnp.bfloat16)
+    for cols in tiles:
+        for rows in parts:
+            d1_ref[rows, cols] = (mm(wmh[rows, :], d2_ref[:, cols]) * s1_ref[rows, cols]).astype(jnp.bfloat16)
+    for cols in tiles:
+        grid_ref[band, cols] = mm(wi_ref[...], d1_ref[:, cols]).astype(jnp.bfloat16)
+    g1[...] += mm_nt(x_ref[...], d1_ref[...])
+    g2[...] += mm_nt(h1_ref[...], d2_ref[...])
+    g3[...] += mm_nt(c_ref[...], h2_ref[...])
 
     @pl.when(n == STEPS - 1)
     def _():
@@ -100,7 +108,8 @@
 
 
 def columns(x, c, wi, wm, wo):
-    block = pl.BlockSpec((FEATURES, TILE), lambda n: (0, n))
+    block = pl.BlockSpec((FEATURES, NLON), lambda n: (0, n))
+    kept = pltpu.VMEM((HIDDEN, NLON), jnp.bfloat16)
     return pl.pallas_call(
         column_kernel,
         grid=(STEPS,),
@@ -117,6 +126,12 @@
             pltpu.VMEM((HIDDEN, FEATURES), jnp.bfloat16),
             pltpu.VMEM((HIDDEN, HIDDEN), jnp.bfloat16),
             pltpu.VMEM((HIDDEN, FEATURES), jnp.bfloat16),
+            pltpu.VMEM((HIDDEN, HIDDEN), jnp.bfloat16),
+            kept,
+            kept,
+            kept,
+            kept,
+            pltpu.VMEM((HIDDEN, NLON), jnp.float32),
             pltpu.VMEM((WIDTH, NLON), jnp.bfloat16),
             pltpu.VMEM((FEATURES, HIDDEN), jnp.float32),
             pltpu.VMEM((HIDDEN, HIDDEN), jnp.float32),
@@ -198,7 +213,7 @@
 
 def pack_out(wide_ref, out_ref):
     def body(p, carry):
-        out_ref[p] = wide_ref[pl.ds(pl.multiple_of(ROWS * p, 8), ROWS), :].astype(jnp.bfloat16)
+        out_ref[p] = wide_ref[pl.ds(PITCH * p, ROWS), :].astype(jnp.bfloat16)
         return carry
 
     lax.fori_loop(0, WAYS, body, 0, unroll=4)
@@ -206,7 +221,7 @@
 
 def unpack_in(in_ref, wide_ref):
     def body(p, carry):
-        wide_ref[pl.ds(pl.multiple_of(ROWS * p, 8), ROWS), :] = in_ref[p].astype(jnp.float32)
+        wide_ref[pl.ds(PITCH * p, ROWS), :] = in_ref[p].astype(jnp.float32)
         return carry
 
     lax.fori_loop(0, WAYS, body, 0, unroll=4)
@@ -217,14 +232,14 @@
         piece = mm(table_ref[pl.ds(pl.multiple_of(256 * k, 256), 256), :], x_ref[...])
         for h in range(2):
             for t in range(TILES):
-                wide_ref[pl.ds((2 * k + h) * TILES + t, WAYS, stride=ROWS), :] = piece[
+                wide_ref[pl.ds((2 * k + h) * TILES + t, WAYS, stride=PITCH), :] = piece[
                     WAYS * h : WAYS * (h + 1), LANES * t : LANES * (t + 1)
                 ]
         return carry
 
     lax.fori_loop(0, SLOTS, body, 0)
     for k in range(GRAD_ROWS):
-        wide_ref[pl.ds(DATA_ROWS + k, WAYS, stride=ROWS), :] = grad_ref[WAYS * k : WAYS * (k + 1), :]
+        wide_ref[pl.ds(DATA_ROWS + k, WAYS, stride=PITCH), :] = grad_ref[WAYS * k : WAYS * (k + 1), :]
     pack_out(wide_ref, out_ref)
 
 
@@ -234,7 +249,7 @@
         in_specs=[VMEM] * 3,
         out_specs=VMEM,
         out_shape=jax.ShapeDtypeStruct((WAYS, ROWS, LANES), jnp.bfloat16),
-        scratch_shapes=[pltpu.VMEM((WAYS * ROWS, LANES), jnp.float32)],
+        scratch_shapes=[pltpu.VMEM((WAYS * PITCH, LANES), jnp.float32)],
         compiler_params=params(48),
         name="forward",
     )(x, table, grad)
@@ -247,13 +262,13 @@
     as_copy.start()
     unpack_in(in_ref, wide_ref)
     for k in range(GRAD_ROWS):
-        slab = wide_ref[pl.ds(DATA_ROWS + k, WAYS, stride=ROWS), :]
+        slab = wide_ref[pl.ds(DATA_ROWS + k, WAYS, stride=PITCH), :]
         sums_ref[k : k + 1, :] = jnp.sum(slab, axis=0, keepdims=True)
     lane = lax.broadcasted_iota(jnp.int32, (WAYS, LANES), 1)
 
     def analyse(s, carry):
         for r in range(2):
-            tiles = [wide_ref[pl.ds((2 * s + r) * TILES + t, WAYS, stride=ROWS), :] for t in range(TILES)]
+            tiles = [wide_ref[pl.ds((2 * s + r) * TILES + t, WAYS, stride=PITCH), :] for t in range(TILES)]
             for g in range(2 * SLOTS):
                 t, off = divmod(LEVELS * g, LANES)
                 piece = tiles[t]
@@ -274,7 +289,7 @@
     def solve(k, carry):
         for u in range(16):
             deg = 16 * k + u
-            rows = pl.ds(pl.multiple_of(deg * BANK, 8), BANK)
+            rows = pl.ds(deg * BANK, 24)
             bank_ref[rows, :LEVELS] = mm(bank_ref[rows, :LEVELS].astype(jnp.bfloat16), inv_ref[deg])
         return carry
 
@@ -299,12 +314,12 @@
                 if off + LEVELS > LANES:
                     tiles[t + 1] = piece
             for t in range(TILES):
-                wide_ref[pl.ds((2 * s + r) * TILES + t, WAYS, stride=ROWS), :] = tiles[t]
+                wide_ref[pl.ds((2 * s + r) * TILES + t, WAYS, stride=PITCH), :] = tiles[t]
         return carry
 
     lax.fori_loop(0, SLOTS, synthesise, 0)
     for k in range(GRAD_ROWS):
-        wide_ref[pl.ds(DATA_ROWS + k, WAYS, stride=ROWS), :] = jnp.broadcast_to(sums_ref[k : k + 1, :], (WAYS, LANES))
+        wide_ref[pl.ds(DATA_ROWS + k, WAYS, stride=PITCH), :] = jnp.broadcast_to(sums_ref[k : k + 1, :], (WAYS, LANES))
     pack_out(wide_ref, out_ref)
 
 
@@ -315,7 +330,7 @@
         out_specs=VMEM,
         out_shape=jax.ShapeDtypeStruct((WAYS, ROWS, LANES), jnp.bfloat16),
         scratch_shapes=[
-            pltpu.VMEM((WAYS * ROWS, LANES), jnp.float32),
+            pltpu.VMEM((WAYS * PITCH, LANES), jnp.float32),
             pltpu.VMEM((NLAT, 4 * LANES), jnp.bfloat16),
             pltpu.VMEM((NDEG * BANK, LANES), jnp.float32),
             pltpu.VMEM((NDEG, LEVELS, LEVELS), jnp.bfloat16),
@@ -332,12 +347,12 @@
     unpack_in(in_ref, wide_ref)
     for t in range(TILES):
         for c in range(2 * SLOTS):
-            slab = wide_ref[pl.ds(TILES * c + t, WAYS, stride=ROWS), :]
+            slab = wide_ref[pl.ds(TILES * c + t, WAYS, stride=PITCH), :]
             rows_ref[LANES * t : LANES * (t + 1), WAYS * c : WAYS * (c + 1)] = slab.T.astype(jnp.bfloat16)
     for i in range(SLOTS):
         out_ref[i] = mm(rows_ref[FEATURES * i : FEATURES * (i + 1), :], table_ref[...])
     for k in range(GRAD_ROWS):
-        grad_ref[WAYS * k : WAYS * (k + 1), :] = wide_ref[pl.ds(DATA_ROWS + k, WAYS, stride=ROWS), :]
+        grad_ref[WAYS * k : WAYS * (k + 1), :] = wide_ref[pl.ds(DATA_ROWS + k, WAYS, stride=PITCH), :]
     scale = 1.0 / math.sqrt(NLAT * NLON)
     at = 0
     for g in (g1, g2, g3):
@@ -359,7 +374,7 @@
             jax.ShapeDtypeStruct((FEATURES, HIDDEN), jnp.float32),
         ],
         scratch_shapes=[
-            pltpu.VMEM((WAYS * ROWS, LANES), jnp.float32),
+            pltpu.VMEM((WAYS * PITCH, LANES), jnp.float32),
             pltpu.VMEM((WIDTH, NLON), jnp.bfloat16),
             pltpu.VMEM((GRAD_ROWS * WAYS, LANES), jnp.float32),
         ],
@@ -373,6 +388,7 @@
 
 
 def on_device(x, c, wi, wm, wo, legendre, level_inverse, wave_order):
+    x, c, wi, wm, wo = (pltpu.with_memory_space_constraint(a, pltpu.HBM) for a in (x, c, wi, wm, wo))
     grid, grad = columns(x, c, wi, wm, wo)
     grid, legendre, level_inverse, wave_order = lax.optimization_barrier((grid, legendre, level_inverse, wave_order))
     rows = swap(grid.reshape(8, LONB, WIDTH), "lev").reshape(NLON, WIDTH)

time: 208 us -> 186 us (0.89)
  Pallas kernels: 85.2 us -> 67 us
  local copies, waits for them, and re-layouts: 30.3 us -> 27 us
    pallas_call x1, Pallas kernels: 36.2 us -> 19.3 us  [columns(): pl.pallas_call(column_kernel, grid=(STEPS,), in_specs=[block, block] + [p...]
    unnamed x22 -> x16, local copies, waits for them, and re-layouts: 10 us -> 7 us
  transfers between devices with their start and end apart: 2 -> 2, of which waited for: 2 -> 2; matrix products, arithmetic and copies ran while one was open for 12% -> 13% of each run, Pallas kernels for 5% -> 5%
where the time goes in v1:
time: 186 us
  Pallas kernels  67 us (36%)
  blocking collectives  44 us (24%)
  waiting for transfers between devices  28.6 us (15%)
  local copies, waits for them, and re-layouts  27 us (15%)
  starting transfers between devices  14.4 us (8%)
  other arithmetic  3.64 us (2%)
    all_to_all x1, blocking collectives, swap(): return lax.all_to_all(array, axis, split_axis=0, concat_axis=0, tiled=True)  44 us
    all_to_all x2, waiting for transfers between devices, swap(): return lax.all_to_all(array, axis, split_axis=0, concat_axis=0, tiled=True)  28.6 us
    pallas_call x1, Pallas kernels, spectral(): pl.pallas_call(spectral_kernel, in_specs=[SMEM, VMEM, VMEM, ANY, ANY], ou...  23.7 us
    pallas_call x1, Pallas kernels, columns(): pl.pallas_call(column_kernel, grid=(STEPS,), in_specs=[block, block] + [p...  19.3 us
    optimization_barrier x1, local copies, waits for them, and re-layouts, on_device(): lax.optimization_barrier((grid, legendre, level_inverse, wave_order))  18.8 us
    all_to_all x2, starting transfers between devices, swap(): return lax.all_to_all(array, axis, split_axis=0, concat_axis=0, tiled=True)  14.4 us
    pallas_call x1, Pallas kernels, forward(): pl.pallas_call(forward_kernel, in_specs=[VMEM] * 3, out_specs=VMEM, out_s...  8.36 us
    pallas_call x1, Pallas kernels, legendre_tables(): pl.pallas_call(legendre_kernel, grid_spec=pltpu.PrefetchScalarGridSpec(nu...  7.69 us
  transfers between devices with their start and end apart: 2, of which 2 were waited for; matrix products, arithmetic and copies ran while one was open for 13% of the time, Pallas kernels for 5%

profile of v1, /device:TPU:0, one launch (start us, length us, event | category | flops | bytes accessed | tf_op | source)
XLA Modules:
  0.0 185.5 jit_solution(1611601215965731263)
XLA Ops:
  0.6 19.3 %columns.1 = (bf16[1280,896]{1,0:T(8,128)(2,1)S(1)}, f32[2304,128]{1,0:T(8,128)S(1)}) custom-call(bf16[176,6400]{1,0:T(8,128)(2,1)} %x_ref.1, bf16[176,6400]{1,0:T(8,128)(2,1)} %c_ref.1, bf16[176,384]{1,0:T(8,128)(2,1)} %wi_ref.1, bf16[384,384]{1,0:T(8,128)(2,1)} %wm_ref.1, bf16[176,384]{1,0:T(8,128)(2,1)} %wo_ref.1), custom_call_target="tpu_custom_call" | custom-call | tf_op jit(solution)/shard_map/columns/pallas_call | solution.py:113
  20.0 0.0 copy-start.4
  20.0 1.4 copy-done.4
  21.3 5.5 %all-to-all-start = ((bf16[8,160,896]{2,1,0:T(8,128)(2,1)}), bf16[8,160,896]{2,1,0:T(8,128)(2,1)S(1)}, u32[]{:S(2)}, u32[]{:S(2)}) async-start(bf16[8,160,896]{2,1,0:T(8,128)(2,1)} %bitcast.7), calls=%async_computation | async-start | bytes 4587520 | tf_op jit(solution)/shard_map/all_to_all | solution.py:387
  26.9 0.2 reshape.25
  27.1 0.1 copy.15
  27.2 0.1 fusion.5
  27.3 0.9 copy.16
  28.2 1.4 sine_multiply_fusion
  29.6 2.1 %multiply_sine_fusion = (f32[640,10]{1,0:T(8,128)S(1)}, f32[640,10]{1,0:T(8,128)S(1)}) fusion(f32[640,10]{1,0:T(8,128)} %copy.16), kind=kLoop, calls=%fused_computation.9 | loop fusion | flops 6400 | bytes 76800 | tf_op jit(solution)/shard_map/sin | solution.py:169
  31.7 1.8 waves.1.table_ref
  33.6 1.7 copy-done
  35.3 20.9 %all-to-all-done = bf16[8,160,896]{2,1,0:T(8,128)(2,1)S(1)} async-done(((bf16[8,160,896]{2,1,0:T(8,128)(2,1)}), bf16[8,160,896]{2,1,0:T(8,128)(2,1)S(1)}, u32[]{:S(2)}, u32[]{:S(2)}) %all-to-all-start) | async-done | bytes 2293792 | tf_op jit(solution)/shard_map/all_to_all | solution.py:387
  56.2 8.4 %forward.1 = bf16[128,88,128]{2,1,0:T(8,128)(2,1)} custom-call(bf16[1280,896]{1,0:T(8,128)(2,1)S(1)} %bitcast.6, bf16[1280,1280]{1,0:T(8,128)(2,1)} %copy-done, f32[2304,128]{1,0:T(8,128)S(1)} %get-tuple-element.19.grad_ref), custom_call_target="tpu_custom_call" | custom-call | tf_op jit(solution)/shard_map/forward/pallas_call | solution.py:247
  64.5 8.8 %all-to-all-start.1 = ((bf16[128,88,128]{2,1,0:T(8,128)(2,1)}), bf16[128,88,128]{2,1,0:T(8,128)(2,1)}, u32[]{:S(2)}, u32[]{:S(2)}) async-start(bf16[128,88,128]{2,1,0:T(8,128)(2,1)} %forward.1), calls=%async_computation.1 | async-start | bytes 5767168 | tf_op jit(solution)/shard_map/all_to_all | solution.py:387
  73.4 0.1 dynamic_slice.3.m_ref
  73.5 18.8 %copy.17 = bf16[88,88,640]{1,0,2:T(8,128)(2,1)} copy(bf16[88,88,640]{2,1,0:T(8,128)(2,1)} %param.14) | data formatting | bytes 19824640 | tf_op jit(solution)/shard_map/optimization_barrier | solution.py:393
  92.3 7.7 %legendre.1 = (bf16[5,640,640]{2,1,0:T(8,128)(2,1)S(1)}, bf16[5,640,640]{2,1,0:T(8,128)(2,1)S(1)}) custom-call(s32[5]{0:T(128)S(1)} %dynamic_slice.3.m_ref, bf16[5,320,640]{2,1,0:T(8,128)(2,1)S(1)} %copy-done.5), custom_call_target="tpu_custom_call" | custom-call | tf_op jit(solution)/shard_map/legendre/pallas_call | solution.py:200
  100.0 2.0 %copy-done.2 = bf16[5,640,640]{2,1,0:T(8,128)(2,1)} copy-done((bf16[5,640,640]{2,1,0:T(8,128)(2,1)}, bf16[5,640,640]{2,1,0:T(8,128)(2,1)S(1)}, u32[]{:S(2)}) %copy-start.2) | copy-done | bytes 4096024
  102.0 1.9 %copy-done.3 = bf16[5,640,640]{2,1,0:T(8,128)(2,1)} copy-done((bf16[5,640,640]{2,1,0:T(8,128)(2,1)}, bf16[5,640,640]{2,1,0:T(8,128)(2,1)S(1)}, u32[]{:S(2)}) %copy-start.3) | copy-done | bytes 4096024
  103.9 7.8 %all-to-all-done.1.in_ref = bf16[128,88,128]{2,1,0:T(8,128)(2,1)} async-done(((bf16[128,88,128]{2,1,0:T(8,128)(2,1)}), bf16[128,88,128]{2,1,0:T(8,128)(2,1)}, u32[]{:S(2)}, u32[]{:S(2)}) %all-to-all-start.1) | async-done | bytes 2883616 | tf_op jit(solution)/shard_map/all_to_all | solution.py:387
  111.6 23.7 %spectral.1 = bf16[128,88,128]{2,1,0:T(8,128)(2,1)} custom-call(s32[5]{0:T(128)} %copy-done.6, bf16[128,88,128]{2,1,0:T(8,128)(2,1)} %all-to-all-done.1.in_ref, bf16[5,640,640]{2,1,0:T(8,128)(2,1)} %copy-done.2, bf16[640,88,88]{2,1,0:T(8,128)(2,1)} %bitcast.8, bf16[5,640,640]{2,1,0:T(8,128)(2,1)} %copy-done.3), custom_call_target="tpu_custom_call" | custom-call | tf_op jit(solution)/shard_map/spectral/pallas_call | solution.py:327
  135.4 44.0 %all_to_all.15.in_ref = bf16[128,88,128]{2,1,0:T(8,128)(2,1)S(1)} all-to-all(bf16[128,88,128]{2,1,0:T(8,128)(2,1)} %spectral.1), channel_id=1, replica_groups=mesh['lat'=16,'lev'=8] {'lat','lev'}, dimensions={0} | all-to-all | bytes 5767168 | tf_op jit(solution)/shard_map/all_to_all | solution.py:387
  179.4 6.1 %inverse.1 = (f32[5,176,1280]{2,1,0:T(8,128)}, f32[176,384]{1,0:T(8,128)}, f32[384,384]{1,0:T(8,128)}, f32[176,384]{1,0:T(8,128)}) custom-call(bf16[128,88,128]{2,1,0:T(8,128)(2,1)S(1)} %all_to_all.15.in_ref, bf16[1280,1280]{1,0:T(8,128)(2,1)S(1)} %copy-done.1), custom_call_target="tpu_custom_call" | custom-call | tf_op jit(solution)/shard_map/inverse/pallas_call | solution.py:366
  (12 shorter events, 0.0 us)
Async XLA Ops:
  20.0 1.4 copy-start.4
  21.3 5.6 %copy-start.7 = (s32[640]{0:T(1024)S(1)}, s32[640]{0:T(1024)}, u32[]{:S(2)}) copy-start(s32[640]{0:T(1024)} %param.15) | copy-start | bytes 7684
  21.3 34.8 %all-to-all-start = ((bf16[8,160,896]{2,1,0:T(8,128)(2,1)}), bf16[8,160,896]{2,1,0:T(8,128)(2,1)S(1)}, u32[]{:S(2)}, u32[]{:S(2)}) async-start(bf16[8,160,896]{2,1,0:T(8,128)(2,1)} %bitcast.7), calls=%async_computation | async-start | bytes 4587520 | tf_op jit(solution)/shard_map/all_to_all | solution.py:387
  33.6 1.7 copy-start
  64.5 47.1 %all-to-all-start.1 = ((bf16[128,88,128]{2,1,0:T(8,128)(2,1)}), bf16[128,88,128]{2,1,0:T(8,128)(2,1)}, u32[]{:S(2)}, u32[]{:S(2)}) async-start(bf16[128,88,128]{2,1,0:T(8,128)(2,1)} %forward.1), calls=%async_computation.1 | async-start | bytes 5767168 | tf_op jit(solution)/shard_map/all_to_all | solution.py:387
  73.5 18.8 %copy-start.6 = (s32[5]{0:T(128)}, s32[5]{0:T(128)S(1)}, u32[]{:S(2)}) copy-start(s32[5]{0:T(128)S(1)} %dynamic_slice.3.m_ref) | copy-start | bytes 64
  73.5 18.8 %copy-start.5 = (bf16[5,320,640]{2,1,0:T(8,128)(2,1)S(1)}, bf16[5,320,640]{2,1,0:T(8,128)(2,1)}, u32[]{:S(2)}) copy-start(bf16[5,320,640]{2,1,0:T(8,128)(2,1)} %leg_ref) | copy-start | bytes 6144004
  100.0 2.0 %copy-start.2 = (bf16[5,640,640]{2,1,0:T(8,128)(2,1)}, bf16[5,640,640]{2,1,0:T(8,128)(2,1)S(1)}, u32[]{:S(2)}) copy-start(bf16[5,640,640]{2,1,0:T(8,128)(2,1)S(1)} %get-tuple-element.21.at_ref) | copy-start | bytes 12288004
  102.0 1.9 %copy-start.3 = (bf16[5,640,640]{2,1,0:T(8,128)(2,1)}, bf16[5,640,640]{2,1,0:T(8,128)(2,1)S(1)}, u32[]{:S(2)}) copy-start(bf16[5,640,640]{2,1,0:T(8,128)(2,1)S(1)} %get-tuple-element.23.as_hbm) | copy-start | bytes 12288004
  135.4 44.1 %copy-start.1 = (bf16[1280,1280]{1,0:T(8,128)(2,1)S(1)}, bf16[1280,1280]{1,0:T(8,128)(2,1)}, u32[]{:S(2)}) copy-start(bf16[1280,1280]{1,0:T(8,128)(2,1)} %copy-done) | copy-start | bytes 9830404

commit v2 on v1

--- a/solution.py
+++ b/solution.py
@@ -1,5 +1,4 @@
 import math
-from functools import partial
 
 import jax
 import jax.numpy as jnp
@@ -7,6 +6,7 @@
 from jax.experimental import pallas as pl
 from jax.experimental.pallas import tpu as pltpu
 from jax.sharding import PartitionSpec as P
+
 
 NLAT = 640
 NLON = 1280
@@ -21,14 +21,14 @@
 LANES = 128
 WIDTH = 896
 TILES = WIDTH // LANES
-DATA_ROWS = 2 * SLOTS * TILES
+ROWS = 72
 GRAD_ROWS = 18
-ROWS = DATA_ROWS + GRAD_ROWS
 COLS = 6400
 TILE = 256
 STEPS = COLS // NLON
 BANK = 25
-PITCH = 89
+INV_PARTS = 5
+PITCH = 73
 EVERYWHERE = ("lat", "lev")
 
 VMEM = pl.BlockSpec(memory_space=pltpu.VMEM)
@@ -227,7 +227,7 @@
     lax.fori_loop(0, WAYS, body, 0, unroll=4)
 
 
-def forward_kernel(x_ref, table_ref, grad_ref, out_ref, wide_ref):
+def forward_kernel(x_ref, table_ref, out_ref, wide_ref):
     def body(k, carry):
         piece = mm(table_ref[pl.ds(pl.multiple_of(256 * k, 256), 256), :], x_ref[...])
         for h in range(2):
@@ -238,32 +238,33 @@
         return carry
 
     lax.fori_loop(0, SLOTS, body, 0)
-    for k in range(GRAD_ROWS):
-        wide_ref[pl.ds(DATA_ROWS + k, WAYS, stride=PITCH), :] = grad_ref[WAYS * k : WAYS * (k + 1), :]
     pack_out(wide_ref, out_ref)
 
 
-def forward(x, table, grad):
+def forward(x, table):
     return pl.pallas_call(
         forward_kernel,
-        in_specs=[VMEM] * 3,
+        in_specs=[VMEM] * 2,
         out_specs=VMEM,
         out_shape=jax.ShapeDtypeStruct((WAYS, ROWS, LANES), jnp.bfloat16),
         scratch_shapes=[pltpu.VMEM((WAYS * PITCH, LANES), jnp.float32)],
-        compiler_params=params(48),
+        compiler_params=params(24),
         name="forward",
-    )(x, table, grad)
-
-
-def spectral_kernel(m_ref, in_ref, at_ref, inv_hbm, as_hbm, out_ref, wide_ref, x_ref, bank_ref, inv_ref, as_ref, sums_ref, sems):
-    inv_copy = pltpu.make_async_copy(inv_hbm, inv_ref, sems.at[0])
+    )(x, table)
+
+
+def spectral_kernel(m_ref, in_ref, at_hbm, inv_hbm, as_hbm, out_ref, wide_ref, x_ref, bank_ref, at_ref, inv_ref, as_ref, sems):
+    at_copy = pltpu.make_async_copy(at_hbm, at_ref, sems.at[0])
+    inv_copies = []
+    for k in range(INV_PARTS):
+        part = pl.ds(k * (NDEG // INV_PARTS), NDEG // INV_PARTS)
+        inv_copies.append(pltpu.make_async_copy(inv_hbm.at[part], inv_ref.at[part], sems.at[2 + k]))
     as_copy = pltpu.make_async_copy(as_hbm, as_ref, sems.at[1])
-    inv_copy.start()
+    at_copy.start()
+    for copy in inv_copies:
+        copy.start()
     as_copy.start()
     unpack_in(in_ref, wide_ref)
-    for k in range(GRAD_ROWS):
-        slab = wide_ref[pl.ds(DATA_ROWS + k, WAYS, stride=PITCH), :]
-        sums_ref[k : k + 1, :] = jnp.sum(slab, axis=0, keepdims=True)
     lane = lax.broadcasted_iota(jnp.int32, (WAYS, LANES), 1)
 
     def analyse(s, carry):
@@ -283,8 +284,8 @@
             bank_ref[pl.ds(4 * s + j, NDEG, stride=BANK), :] = y[:, LANES * j : LANES * (j + 1)]
         return carry
 
+    at_copy.wait()
     lax.fori_loop(0, SLOTS, analyse, 0)
-    inv_copy.wait()
 
     def solve(k, carry):
         for u in range(16):
@@ -293,8 +294,10 @@
             bank_ref[rows, :LEVELS] = mm(bank_ref[rows, :LEVELS].astype(jnp.bfloat16), inv_ref[deg])
         return carry
 
-    lax.fori_loop(0, NDEG // 16, solve, 0)
-    as_copy.wait()
+    steps = NDEG // 16 // INV_PARTS
+    for k, copy in enumerate(inv_copies):
+        copy.wait()
+        lax.fori_loop(steps * k, steps * (k + 1), solve, 0)
 
     def synthesise(s, carry):
         z = jnp.concatenate(
@@ -317,33 +320,32 @@
                 wide_ref[pl.ds((2 * s + r) * TILES + t, WAYS, stride=PITCH), :] = tiles[t]
         return carry
 
+    as_copy.wait()
     lax.fori_loop(0, SLOTS, synthesise, 0)
-    for k in range(GRAD_ROWS):
-        wide_ref[pl.ds(DATA_ROWS + k, WAYS, stride=PITCH), :] = jnp.broadcast_to(sums_ref[k : k + 1, :], (WAYS, LANES))
     pack_out(wide_ref, out_ref)
 
 
 def spectral(wave_local, arrived, at, inv, synth):
     return pl.pallas_call(
         spectral_kernel,
-        in_specs=[SMEM, VMEM, VMEM, ANY, ANY],
+        in_specs=[SMEM, VMEM, ANY, ANY, ANY],
         out_specs=VMEM,
         out_shape=jax.ShapeDtypeStruct((WAYS, ROWS, LANES), jnp.bfloat16),
         scratch_shapes=[
             pltpu.VMEM((WAYS * PITCH, LANES), jnp.float32),
             pltpu.VMEM((NLAT, 4 * LANES), jnp.bfloat16),
             pltpu.VMEM((NDEG * BANK, LANES), jnp.float32),
+            pltpu.VMEM((SLOTS, NDEG, NLAT), jnp.bfloat16),
             pltpu.VMEM((NDEG, LEVELS, LEVELS), jnp.bfloat16),
             pltpu.VMEM((SLOTS, NLAT, NDEG), jnp.bfloat16),
-            pltpu.VMEM((24, LANES), jnp.float32),
-            pltpu.SemaphoreType.DMA((2,)),
+            pltpu.SemaphoreType.DMA((2 + INV_PARTS,)),
         ],
-        compiler_params=params(58),
+        compiler_params=params(46),
         name="spectral",
     )(wave_local, arrived, at, inv, synth)
 
 
-def inverse_kernel(in_ref, table_ref, out_ref, g1, g2, g3, wide_ref, rows_ref, grad_ref):
+def inverse_kernel(in_ref, table_ref, out_ref, wide_ref, rows_ref):
     unpack_in(in_ref, wide_ref)
     for t in range(TILES):
         for c in range(2 * SLOTS):
@@ -351,54 +353,99 @@
             rows_ref[LANES * t : LANES * (t + 1), WAYS * c : WAYS * (c + 1)] = slab.T.astype(jnp.bfloat16)
     for i in range(SLOTS):
         out_ref[i] = mm(rows_ref[FEATURES * i : FEATURES * (i + 1), :], table_ref[...])
-    for k in range(GRAD_ROWS):
-        grad_ref[WAYS * k : WAYS * (k + 1), :] = wide_ref[pl.ds(DATA_ROWS + k, WAYS, stride=PITCH), :]
+
+
+def inverse(arrived, table):
+    return pl.pallas_call(
+        inverse_kernel,
+        in_specs=[VMEM] * 2,
+        out_specs=VMEM,
+        out_shape=jax.ShapeDtypeStruct((SLOTS, FEATURES, NLON), jnp.float32),
+        scratch_shapes=[
+            pltpu.VMEM((WAYS * PITCH, LANES), jnp.float32),
+            pltpu.VMEM((WIDTH, NLON), jnp.bfloat16),
+        ],
+        compiler_params=params(28),
+        name="inverse",
+    )(arrived, table)
+
+
+def unstack_kernel(in_ref, g1, g2, g3):
     scale = 1.0 / math.sqrt(NLAT * NLON)
     at = 0
     for g in (g1, g2, g3):
         rows = g.shape[0]
         for t in range(HIDDEN // LANES):
-            g[:, LANES * t : LANES * (t + 1)] = grad_ref[at : at + rows, :] * scale
+            g[:, LANES * t : LANES * (t + 1)] = in_ref[at : at + rows, :].astype(jnp.float32) * scale
             at += rows
 
 
-def inverse(arrived, table):
-    return pl.pallas_call(
-        inverse_kernel,
-        in_specs=[VMEM] * 2,
-        out_specs=[VMEM] * 4,
-        out_shape=[
-            jax.ShapeDtypeStruct((SLOTS, FEATURES, NLON), jnp.float32),
-            jax.ShapeDtypeStruct((FEATURES, HIDDEN), jnp.float32),
-            jax.ShapeDtypeStruct((HIDDEN, HIDDEN), jnp.float32),
-            jax.ShapeDtypeStruct((FEATURES, HIDDEN), jnp.float32),
-        ],
-        scratch_shapes=[
-            pltpu.VMEM((WAYS * PITCH, LANES), jnp.float32),
-            pltpu.VMEM((WIDTH, NLON), jnp.bfloat16),
-            pltpu.VMEM((GRAD_ROWS * WAYS, LANES), jnp.float32),
-        ],
-        compiler_params=params(48),
-        name="inverse",
-    )(arrived, table)
+def unstack(grad):
+    return pl.pallas_call(
+        unstack_kernel,
+        in_specs=[VMEM],
+        out_specs=[VMEM] * 3,
+        out_shape=[jax.ShapeDtypeStruct((r, HIDDEN), jnp.float32) for r in (FEATURES, HIDDEN, FEATURES)],
+        compiler_params=params(8),
+        name="unstack",
+    )(grad)
+
+
+STAGES = (("lev", 1), ("lat", 1), ("lat", 4), ("lat", 2), ("lat", 8), ("lev", 2), ("lev", 4))
+EARLY = 4
+
+
+def across(array, axis, bit):
+    size = lax.axis_size(axis)
+    return lax.ppermute(array, axis, [(i, i ^ bit) for i in range(size)])
+
+
+def upper(axis, bit):
+    return (lax.axis_index(axis) & bit) != 0
+
+
+def halve(total, axis, bit):
+    half = total.shape[0] // 2
+    low, high = total[:half], total[half:]
+    mine = upper(axis, bit)
+    sent = jnp.where(mine, low, high).astype(jnp.bfloat16)
+    return jnp.where(mine, high, low) + across(sent, axis, bit).astype(jnp.float32)
+
+
+def double(part, axis, bit):
+    other = across(part, axis, bit)
+    mine = upper(axis, bit)
+    return jnp.concatenate([jnp.where(mine, other, part), jnp.where(mine, part, other)])
 
 
 def swap(array, axis):
     return lax.all_to_all(array, axis, split_axis=0, concat_axis=0, tiled=True)
 
 
-def on_device(x, c, wi, wm, wo, legendre, level_inverse, wave_order):
+def program(x, c, wi, wm, wo, legendre, level_inverse, wave_order):
     x, c, wi, wm, wo = (pltpu.with_memory_space_constraint(a, pltpu.HBM) for a in (x, c, wi, wm, wo))
     grid, grad = columns(x, c, wi, wm, wo)
     grid, legendre, level_inverse, wave_order = lax.optimization_barrier((grid, legendre, level_inverse, wave_order))
-    rows = swap(grid.reshape(8, LONB, WIDTH), "lev").reshape(NLON, WIDTH)
+    rows = swap(grid.reshape(8, LONB, WIDTH), "lev")
+    rows = rows.reshape(NLON, WIDTH)
     wave_local = lax.dynamic_slice_in_dim(wave_order, lax.axis_index(EVERYWHERE) * SLOTS, SLOTS)
     table = wave_table(wave_order)
+    for axis, bit in STAGES[:EARLY]:
+        grad = halve(grad, axis, bit)
+    rows, table, grad = lax.optimization_barrier((rows, table, grad))
     at, synth = legendre_tables(wave_local, legendre)
     inv = level_inverse.transpose(2, 0, 1)
-    arrived = swap(forward(rows, table, grad), EVERYWHERE)
-    arrived = swap(spectral(wave_local, arrived, at, inv, synth), EVERYWHERE)
-    out, g1, g2, g3 = inverse(arrived, table)
+    arrived = swap(forward(rows, table), EVERYWHERE)
+    zonal = spectral(wave_local, arrived, at, inv, synth)
+    zonal, grad = lax.optimization_barrier((zonal, grad))
+    for axis, bit in STAGES[EARLY:]:
+        grad = halve(grad, axis, bit)
+    grad = grad.astype(jnp.bfloat16)
+    for axis, bit in STAGES[::-1]:
+        grad = double(grad, axis, bit)
+    g1, g2, g3 = unstack(grad)
+    arrived = swap(zonal, EVERYWHERE)
+    out = inverse(arrived, table)
     return g1, g2, g3, out.transpose(1, 0, 2)
 
 
@@ -414,4 +461,4 @@
         P(),
     )
     out_specs = (P(), P(), P(), P(None, EVERYWHERE, None))
-    return jax.shard_map(on_device, mesh=mesh, in_specs=in_specs, out_specs=out_specs, check_vma=False)
+    return jax.shard_map(program, mesh=mesh, in_specs=in_specs, out_specs=out_specs, check_vma=False)

time: 186 us -> 215 us (1.16)
  blocking collectives: 44 us -> 0 us
  waiting for transfers between devices: 28.6 us -> 68.2 us
  starting transfers between devices: 14.4 us -> 42.1 us
  local copies, waits for them, and re-layouts: 27 us -> 31.9 us
    ppermute x0 -> x14, waiting for transfers between devices: none -> 57.7 us  [across(): return lax.ppermute(array, axis, [(i, i ^ bit) for i in range(size)])]
    all_to_all x1 -> x0, blocking collectives: 44 us -> none  [swap(): return lax.all_to_all(array, axis, split_axis=0, concat_axis=0, tiled=True)]
    ppermute x0 -> x14, starting transfers between devices: none -> 18.7 us  [across(): return lax.ppermute(array, axis, [(i, i ^ bit) for i in range(size)])]
    all_to_all x2 -> x3, waiting for transfers between devices: 28.6 us -> 10.5 us  [swap(): return lax.all_to_all(array, axis, split_axis=0, concat_axis=0, tiled=True)]
    all_to_all x2 -> x3, starting transfers between devices: 14.4 us -> 23.4 us  [swap(): return lax.all_to_all(array, axis, split_axis=0, concat_axis=0, tiled=True)]
    unnamed x16 -> x22, local copies, waits for them, and re-layouts: 7 us -> 12.7 us
    pallas_call x3 -> x4, Pallas kernels: 38.2 us -> 36.8 us  [the longest x1 22.1 us: spectral(): pl.pallas_call(spectral_kernel, in_specs=[SMEM, VMEM, ANY, ANY, ANY], out...]
  transfers between devices with their start and end apart: 2 -> 17, of which waited for: 2 -> 13; matrix products, arithmetic and copies ran while one was open for 13% -> 11% of each run, Pallas kernels for 5% -> 5%
where the time goes in v2:
time: 215 us; the launch traced here: 213 us
  waiting for transfers between devices  68.2 us (32%)
  Pallas kernels  65.6 us (31%)
  starting transfers between devices  42.1 us (20%)
  local copies, waits for them, and re-layouts  31.9 us (15%)
  other arithmetic  4.1 us (2%)
    ppermute x14, waiting for transfers between devices, across(): return lax.ppermute(array, axis, [(i, i ^ bit) for i in range(size)])  57.7 us
    all_to_all x3, starting transfers between devices, swap(): return lax.all_to_all(array, axis, split_axis=0, concat_axis=0, tiled=True)  23.4 us
    pallas_call x1, Pallas kernels, spectral(): pl.pallas_call(spectral_kernel, in_specs=[SMEM, VMEM, ANY, ANY, ANY], out...  22.1 us
    pallas_call x1, Pallas kernels, columns(): pl.pallas_call(column_kernel, grid=(STEPS,), in_specs=[block, block] + [p...  19.3 us
    optimization_barrier x1, local copies, waits for them, and re-layouts, program(): lax.optimization_barrier((grid, legendre, level_inverse, wave_order))  18.7 us
    ppermute x14, starting transfers between devices, across(): return lax.ppermute(array, axis, [(i, i ^ bit) for i in range(size)])  18.7 us
    unnamed x22, local copies, waits for them, and re-layouts  12.7 us
    all_to_all x3, waiting for transfers between devices, swap(): return lax.all_to_all(array, axis, split_axis=0, concat_axis=0, tiled=True)  10.5 us
  transfers between devices with their start and end apart: 17, of which 13 were waited for; matrix products, arithmetic and copies ran while one was open for 11% of the time, Pallas kernels for 5%

profile of v2, /device:TPU:0, one launch (start us, length us, event | category | flops | bytes accessed | tf_op | source)
XLA Modules:
  0.0 212.7 jit_solution(15608555439953039913)
XLA Ops:
  0.6 19.3 %columns.1 = (bf16[1280,896]{1,0:T(8,128)(2,1)S(1)}, f32[2304,128]{1,0:T(8,128)S(1)}) custom-call(bf16[176,6400]{1,0:T(8,128)(2,1)} %x_ref.1, bf16[176,6400]{1,0:T(8,128)(2,1)} %c_ref.1, bf16[176,384]{1,0:T(8,128)(2,1)} %wi_ref.1, bf16[384,384]{1,0:T(8,128)(2,1)} %wm_ref.1, bf16[176,384]{1,0:T(8,128)(2,1)} %wo_ref.1), custom_call_target="tpu_custom_call" | custom-call | tf_op jit(solution)/shard_map/columns/pallas_call | solution.py:113
  22.5 5.6 %all-to-all-start = ((bf16[8,160,896]{2,1,0:T(8,128)(2,1)}), bf16[8,160,896]{2,1,0:T(8,128)(2,1)}, u32[]{:S(2)}, u32[]{:S(2)}) async-start(bf16[8,160,896]{2,1,0:T(8,128)(2,1)} %bitcast.6), calls=%async_computation | async-start | bytes 4587520 | tf_op jit(solution)/shard_map/all_to_all | solution.py:422
  30.4 4.5 %collective-permute-done.1 = bf16[576,128]{1,0:T(8,128)(2,1)S(1)} collective-permute-done((bf16[576,128]{1,0:T(8,128)(2,1)S(1)}, bf16[576,128]{1,0:T(8,128)(2,1)S(1)}, u32[]{:S(2)}, u32[]{:S(2)}) %collective-permute-start.1) | collective-permute-done | bytes 147488 | tf_op jit(solution)/shard_map/ppermute | solution.py:400
  39.5 3.1 %collective-permute-start.3 = (bf16[144,128]{1,0:T(8,128)(2,1)S(1)}, bf16[144,128]{1,0:T(8,128)(2,1)S(1)}, u32[]{:S(2)}, u32[]{:S(2)}) collective-permute-start(bf16[144,128]{1,0:T(8,128)(2,1)S(1)} %select_convert_fusion.3), channel_id=1, source_target_pairs={{0,16},{8,24},{16,0},{24,8},{32,48},{40,56},{48,32},{56,40},{64,80... | collective-permute-start | bytes 110600 | tf_op jit(solution)/shard_map/ppermute | solution.py:400
  47.8 9.7 %all-to-all-done = bf16[8,160,896]{2,1,0:T(8,128)(2,1)} async-done(((bf16[8,160,896]{2,1,0:T(8,128)(2,1)}), bf16[8,160,896]{2,1,0:T(8,128)(2,1)}, u32[]{:S(2)}, u32[]{:S(2)}) %all-to-all-start) | async-done | bytes 2293792 | tf_op jit(solution)/shard_map/all_to_all | solution.py:422
  57.6 6.2 %forward.1 = bf16[128,72,128]{2,1,0:T(8,128)(2,1)S(1)} custom-call(bf16[1280,896]{1,0:T(8,128)(2,1)} %bitcast.1.x_ref, bf16[1280,1280]{1,0:T(8,128)(2,1)S(1)} %waves.1.table_ref), custom_call_target="tpu_custom_call" | custom-call | tf_op jit(solution)/shard_map/forward/pallas_call | solution.py:245
  65.2 8.8 %all-to-all-start.1 = ((bf16[128,72,128]{2,1,0:T(8,128)(2,1)}), bf16[128,72,128]{2,1,0:T(8,128)(2,1)}, u32[]{:S(2)}, u32[]{:S(2)}) async-start(bf16[128,72,128]{2,1,0:T(8,128)(2,1)} %copy-done.1), calls=%async_computation.1 | async-start | bytes 4718592 | tf_op jit(solution)/shard_map/all_to_all | solution.py:422
  74.2 18.7 %copy.17 = bf16[88,88,640]{1,0,2:T(8,128)(2,1)} copy(bf16[88,88,640]{2,1,0:T(8,128)(2,1)} %param.14) | data formatting | bytes 19824640 | tf_op jit(solution)/shard_map/optimization_barrier | solution.py:428
  94.4 7.6 %legendre.1 = (bf16[5,640,640]{2,1,0:T(8,128)(2,1)S(1)}, bf16[5,640,640]{2,1,0:T(8,128)(2,1)S(1)}) custom-call(s32[5]{0:T(128)S(1)} %dynamic_slice.3.m_ref, bf16[5,320,640]{2,1,0:T(8,128)(2,1)S(1)} %copy-done.7), custom_call_target="tpu_custom_call" | custom-call | tf_op jit(solution)/shard_map/legendre/pallas_call | solution.py:200
  102.1 2.0 copy-done.2
  104.1 1.9 copy-done.3
  106.7 22.1 %spectral.1 = bf16[128,72,128]{2,1,0:T(8,128)(2,1)S(1)} custom-call(s32[5]{0:T(128)S(1)} %dynamic_slice.3.m_ref, bf16[128,72,128]{2,1,0:T(8,128)(2,1)} %all-to-all-done.1.in_ref, bf16[5,640,640]{2,1,0:T(8,128)(2,1)} %copy-done.2, bf16[640,88,88]{2,1,0:T(8,128)(2,1)} %bitcast.7, bf16[5,640,640]{2,1,0:T(8,128)(2,1)} %copy-done.3), custom_call_target="tpu_custom_call" | custom-call | tf_op jit(solution)/shard_map/spectral/pallas_call | solution.py:329
  131.8 3.8 %collective-permute-done.4 = bf16[72,128]{1,0:T(8,128)(2,1)S(1)} collective-permute-done((bf16[72,128]{1,0:T(8,128)(2,1)S(1)}, bf16[72,128]{1,0:T(8,128)(2,1)S(1)}, u32[]{:S(2)}, u32[]{:S(2)}) %collective-permute-start.4) | collective-permute-done | bytes 18464 | tf_op jit(solution)/shard_map/ppermute | solution.py:400
  135.9 3.5 %collective-permute-done.5 = bf16[36,128]{1,0:T(8,128)(2,1)S(1)} collective-permute-done((bf16[36,128]{1,0:T(8,128)(2,1)S(1)}, bf16[36,128]{1,0:T(8,128)(2,1)S(1)}, u32[]{:S(2)}, u32[]{:S(2)}) %collective-permute-start.5) | collective-permute-done | bytes 9248 | tf_op jit(solution)/shard_map/ppermute | solution.py:400
  139.4 2.0 collective-permute-start.6
  141.4 3.2 %collective-permute-done.6 = bf16[18,128]{1,0:T(8,128)(2,1)S(1)} collective-permute-done((bf16[18,128]{1,0:T(8,128)(2,1)S(1)}, bf16[18,128]{1,0:T(8,128)(2,1)S(1)}, u32[]{:S(2)}, u32[]{:S(2)}) %collective-permute-start.6) | collective-permute-done | bytes 4640 | tf_op jit(solution)/shard_map/ppermute | solution.py:400
  146.5 3.2 %collective-permute-done.7 = bf16[18,128]{1,0:T(8,128)(2,1)S(1)} collective-permute-done((bf16[18,128]{1,0:T(8,128)(2,1)S(1)}, bf16[18,128]{1,0:T(8,128)(2,1)S(1)}, u32[]{:S(2)}, u32[]{:S(2)}) %collective-permute-start.7) | collective-permute-done | bytes 4640 | tf_op jit(solution)/shard_map/ppermute | solution.py:400
  150.1 3.5 %collective-permute-done.8 = bf16[36,128]{1,0:T(8,128)(2,1)S(1)} collective-permute-done((bf16[36,128]{1,0:T(8,128)(2,1)S(1)}, bf16[36,128]{1,0:T(8,128)(2,1)S(1)}, u32[]{:S(2)}, u32[]{:S(2)}) %collective-permute-start.8) | collective-permute-done | bytes 9248 | tf_op jit(solution)/shard_map/ppermute | solution.py:400
  155.1 3.8 %collective-permute-done.9 = bf16[72,128]{1,0:T(8,128)(2,1)S(1)} collective-permute-done((bf16[72,128]{1,0:T(8,128)(2,1)S(1)}, bf16[72,128]{1,0:T(8,128)(2,1)S(1)}, u32[]{:S(2)}, u32[]{:S(2)}) %collective-permute-start.9) | collective-permute-done | bytes 18464 | tf_op jit(solution)/shard_map/ppermute | solution.py:400
  160.5 8.9 %all-to-all-start.2 = ((bf16[128,72,128]{2,1,0:T(8,128)(2,1)}), bf16[128,72,128]{2,1,0:T(8,128)(2,1)}, u32[]{:S(2)}, u32[]{:S(2)}) async-start(bf16[128,72,128]{2,1,0:T(8,128)(2,1)} %copy-done), calls=%async_computation.2 | async-start | bytes 4718592 | tf_op jit(solution)/shard_map/all_to_all | solution.py:422
  170.5 26.0 %collective-permute-done.11 = bf16[288,128]{1,0:T(8,128)(2,1)S(1)} collective-permute-done((bf16[288,128]{1,0:T(8,128)(2,1)S(1)}, bf16[288,128]{1,0:T(8,128)(2,1)S(1)}, u32[]{:S(2)}, u32[]{:S(2)}) %collective-permute-start.11) | collective-permute-done | bytes 73760 | tf_op jit(solution)/shard_map/ppermute | solution.py:400
  196.5 2.0 collective-permute-start.12
  198.5 3.8 %collective-permute-done.12 = bf16[576,128]{1,0:T(8,128)(2,1)S(1)} collective-permute-done((bf16[576,128]{1,0:T(8,128)(2,1)S(1)}, bf16[576,128]{1,0:T(8,128)(2,1)S(1)}, u32[]{:S(2)}, u32[]{:S(2)}) %collective-permute-start.12) | collective-permute-done | bytes 147488 | tf_op jit(solution)/shard_map/ppermute | solution.py:400
  205.3 7.4 %inverse.1 = f32[5,176,1280]{2,1,0:T(8,128)} custom-call(bf16[128,72,128]{2,1,0:T(8,128)(2,1)} %all-to-all-done.2.in_ref, bf16[1280,1280]{1,0:T(8,128)(2,1)S(1)} %waves.1.table_ref), custom_call_target="tpu_custom_call" | custom-call | tf_op jit(solution)/shard_map/inverse/pallas_call | solution.py:359
  (76 shorter events, 31.1 us)
Async XLA Ops:
  22.4 6.0 %collective-permute-start = (bf16[1152,128]{1,0:T(8,128)(2,1)S(1)}, bf16[1152,128]{1,0:T(8,128)(2,1)S(1)}, u32[]{:S(2)}, u32[]{:S(2)}) collective-permute-start(bf16[1152,128]{1,0:T(8,128)(2,1)S(1)} %select_convert_fusion), channel_id=1, source_target_pairs={{0,1},{1,0},{2,3},{3,2},{4,5},{5,4},{6,7},{7,6},{8,9},{9,8},{10,11... | collective-permute-start | bytes 884744 | tf_op jit(solution)/shard_map/ppermute | solution.py:400
  22.5 5.7 %copy-start.10 = (s32[640]{0:T(1024)S(1)}, s32[640]{0:T(1024)}, u32[]{:S(2)}) copy-start(s32[640]{0:T(1024)} %param.15) | copy-start | bytes 7684
  22.5 5.9 %copy-start.5 = (f32[2304,128]{1,0:T(8,128)S(1)}, f32[2304,128]{1,0:T(8,128)}, u32[]{:S(2)}) copy-start(f32[2304,128]{1,0:T(8,128)} %copy-done.4) | copy-start | bytes 3538948
  22.5 35.0 %all-to-all-start = ((bf16[8,160,896]{2,1,0:T(8,128)(2,1)}), bf16[8,160,896]{2,1,0:T(8,128)(2,1)}, u32[]{:S(2)}, u32[]{:S(2)}) async-start(bf16[8,160,896]{2,1,0:T(8,128)(2,1)} %bitcast.6), calls=%async_computation | async-start | bytes 4587520 | tf_op jit(solution)/shard_map/all_to_all | solution.py:422
  28.6 6.3 %collective-permute-start.1 = (bf16[576,128]{1,0:T(8,128)(2,1)S(1)}, bf16[576,128]{1,0:T(8,128)(2,1)S(1)}, u32[]{:S(2)}, u32[]{:S(2)}) collective-permute-start(bf16[576,128]{1,0:T(8,128)(2,1)S(1)} %select_convert_fusion.1), channel_id=1, source_target_pairs={{0,8},{8,0},{16,24},{24,16},{32,40},{40,32},{48,56},{56,48},{64,72... | collective-permute-start | bytes 442376 | tf_op jit(solution)/shard_map/ppermute | solution.py:400
  35.0 4.4 %collective-permute-start.2 = (bf16[288,128]{1,0:T(8,128)(2,1)S(1)}, bf16[288,128]{1,0:T(8,128)(2,1)S(1)}, u32[]{:S(2)}, u32[]{:S(2)}) collective-permute-start(bf16[288,128]{1,0:T(8,128)(2,1)S(1)} %select_convert_fusion.2), channel_id=1, source_target_pairs={{0,32},{8,40},{16,48},{24,56},{32,0},{40,8},{48,16},{56,24},{64,96... | collective-permute-start | bytes 221192 | tf_op jit(solution)/shard_map/ppermute | solution.py:400
  39.5 8.3 %collective-permute-start.3 = (bf16[144,128]{1,0:T(8,128)(2,1)S(1)}, bf16[144,128]{1,0:T(8,128)(2,1)S(1)}, u32[]{:S(2)}, u32[]{:S(2)}) collective-permute-start(bf16[144,128]{1,0:T(8,128)(2,1)S(1)} %select_convert_fusion.3), channel_id=1, source_target_pairs={{0,16},{8,24},{16,0},{24,8},{32,48},{40,56},{48,32},{56,40},{64,80... | collective-permute-start | bytes 110600 | tf_op jit(solution)/shard_map/ppermute | solution.py:400
  63.8 1.4 copy-start.1
  65.2 41.5 %all-to-all-start.1 = ((bf16[128,72,128]{2,1,0:T(8,128)(2,1)}), bf16[128,72,128]{2,1,0:T(8,128)(2,1)}, u32[]{:S(2)}, u32[]{:S(2)}) async-start(bf16[128,72,128]{2,1,0:T(8,128)(2,1)} %copy-done.1), calls=%async_computation.1 | async-start | bytes 4718592 | tf_op jit(solution)/shard_map/all_to_all | solution.py:422
  92.9 1.6 copy-start.7
  102.1 2.0 copy-start.2
  104.1 1.9 copy-start.3
  128.8 1.4 copy-start
  130.2 5.3 %collective-permute-start.4 = (bf16[72,128]{1,0:T(8,128)(2,1)S(1)}, bf16[72,128]{1,0:T(8,128)(2,1)S(1)}, u32[]{:S(2)}, u32[]{:S(2)}) collective-permute-start(bf16[72,128]{1,0:T(8,128)(2,1)S(1)} %select_convert_fusion.4), channel_id=1, source_target_pairs={{0,64},{8,72},{16,80},{24,88},{32,96},{40,104},{48,112},{56,120},{... | collective-permute-start | bytes 55304 | tf_op jit(solution)/shard_map/ppermute | solution.py:400
  135.6 3.8 %collective-permute-start.5 = (bf16[36,128]{1,0:T(8,128)(2,1)S(1)}, bf16[36,128]{1,0:T(8,128)(2,1)S(1)}, u32[]{:S(2)}, u32[]{:S(2)}) collective-permute-start(bf16[36,128]{1,0:T(8,128)(2,1)S(1)} %select_convert_fusion.5), channel_id=1, source_target_pairs={{0,2},{1,3},{2,0},{3,1},{4,6},{5,7},{6,4},{7,5},{8,10},{9,11},{10,... | collective-permute-start | bytes 27656 | tf_op jit(solution)/shard_map/ppermute | solution.py:400
  139.4 5.2 %collective-permute-start.6 = (bf16[18,128]{1,0:T(8,128)(2,1)S(1)}, bf16[18,128]{1,0:T(8,128)(2,1)S(1)}, u32[]{:S(2)}, u32[]{:S(2)}) collective-permute-start(bf16[18,128]{1,0:T(8,128)(2,1)S(1)} %select_convert_fusion.6), channel_id=1, source_target_pairs={{0,4},{1,5},{2,6},{3,7},{4,0},{5,1},{6,2},{7,3},{8,12},{9,13},{10,... | collective-permute-start | bytes 13832 | tf_op jit(solution)/shard_map/ppermute | solution.py:400
  144.6 5.1 %collective-permute-start.7 = (bf16[18,128]{1,0:T(8,128)(2,1)S(1)}, bf16[18,128]{1,0:T(8,128)(2,1)S(1)}, u32[]{:S(2)}, u32[]{:S(2)}) collective-permute-start(bf16[18,128]{1,0:T(8,128)(2,1)S(1)} %add_convert_fusion), channel_id=1, source_target_pairs={{0,4},{1,5},{2,6},{3,7},{4,0},{5,1},{6,2},{7,3},{8,12},{9,13},{10,... | collective-permute-start | bytes 13832 | tf_op jit(solution)/shard_map/ppermute | solution.py:400
  149.8 3.8 %collective-permute-start.8 = (bf16[36,128]{1,0:T(8,128)(2,1)S(1)}, bf16[36,128]{1,0:T(8,128)(2,1)S(1)}, u32[]{:S(2)}, u32[]{:S(2)}) collective-permute-start(bf16[36,128]{1,0:T(8,128)(2,1)S(1)} %pad_maximum_fusion.6), channel_id=1, source_target_pairs={{0,2},{1,3},{2,0},{3,1},{4,6},{5,7},{6,4},{7,5},{8,10},{9,11},{10,... | collective-permute-start | bytes 27656 | tf_op jit(solution)/shard_map/ppermute | solution.py:400
  153.5 5.3 %collective-permute-start.9 = (bf16[72,128]{1,0:T(8,128)(2,1)S(1)}, bf16[72,128]{1,0:T(8,128)(2,1)S(1)}, u32[]{:S(2)}, u32[]{:S(2)}) collective-permute-start(bf16[72,128]{1,0:T(8,128)(2,1)S(1)} %pad_maximum_fusion.5), channel_id=1, source_target_pairs={{0,64},{8,72},{16,80},{24,88},{32,96},{40,104},{48,112},{56,120},{... | collective-permute-start | bytes 55304 | tf_op jit(solution)/shard_map/ppermute | solution.py:400
  158.9 10.5 %collective-permute-start.10 = (bf16[144,128]{1,0:T(8,128)(2,1)S(1)}, bf16[144,128]{1,0:T(8,128)(2,1)S(1)}, u32[]{:S(2)}, u32[]{:S(2)}) collective-permute-start(bf16[144,128]{1,0:T(8,128)(2,1)S(1)} %pad_maximum_fusion.4), channel_id=1, source_target_pairs={{0,16},{8,24},{16,0},{24,8},{32,48},{40,56},{48,32},{56,40},{64,80... | collective-permute-start | bytes 110600 | tf_op jit(solution)/shard_map/ppermute | solution.py:400
  160.5 44.8 %all-to-all-start.2 = ((bf16[128,72,128]{2,1,0:T(8,128)(2,1)}), bf16[128,72,128]{2,1,0:T(8,128)(2,1)}, u32[]{:S(2)}, u32[]{:S(2)}) async-start(bf16[128,72,128]{2,1,0:T(8,128)(2,1)} %copy-done), calls=%async_computation.2 | async-start | bytes 4718592 | tf_op jit(solution)/shard_map/all_to_all | solution.py:422
  169.5 27.0 %collective-permute-start.11 = (bf16[288,128]{1,0:T(8,128)(2,1)S(1)}, bf16[288,128]{1,0:T(8,128)(2,1)S(1)}, u32[]{:S(2)}, u32[]{:S(2)}) collective-permute-start(bf16[288,128]{1,0:T(8,128)(2,1)S(1)} %pad_maximum_fusion.3), channel_id=1, source_target_pairs={{0,32},{8,40},{16,48},{24,56},{32,0},{40,8},{48,16},{56,24},{64,96... | collective-permute-start | bytes 221192 | tf_op jit(solution)/shard_map/ppermute | solution.py:400
  196.5 5.8 %collective-permute-start.12 = (bf16[576,128]{1,0:T(8,128)(2,1)S(1)}, bf16[576,128]{1,0:T(8,128)(2,1)S(1)}, u32[]{:S(2)}, u32[]{:S(2)}) collective-permute-start(bf16[576,128]{1,0:T(8,128)(2,1)S(1)} %pad_maximum_fusion.2), channel_id=1, source_target_pairs={{0,8},{8,0},{16,24},{24,16},{32,40},{40,32},{48,56},{56,48},{64,72... | collective-permute-start | bytes 442376 | tf_op jit(solution)/shard_map/ppermute | solution.py:400
  202.4 1.7 collective-permute-start.13
  (4 other events, 4.4 us)

commit v3 on v2

--- a/solution.py
+++ b/solution.py
@@ -21,19 +21,27 @@
 LANES = 128
 WIDTH = 896
 TILES = WIDTH // LANES
+DATA_ROWS = 2 * SLOTS * TILES
 ROWS = 72
+LATE_ROWS = 88
 GRAD_ROWS = 18
+BLOCKS = 32
+BLOCK_ROWS = 72
 COLS = 6400
 TILE = 256
 STEPS = COLS // NLON
 BANK = 25
 INV_PARTS = 5
 PITCH = 73
+LATE_PITCH = 89
 EVERYWHERE = ("lat", "lev")
 
 VMEM = pl.BlockSpec(memory_space=pltpu.VMEM)
 SMEM = pl.BlockSpec(memory_space=pltpu.SMEM)
 ANY = pl.BlockSpec(memory_space=pl.ANY)
+HBM = pl.BlockSpec(memory_space=pltpu.HBM)
+GROUPS = 8
+GROUP = WAYS // GROUPS
 
 
 def mm(left, right):
@@ -52,7 +60,7 @@
     return pltpu.CompilerParams(vmem_limit_bytes=mib * 1024 * 1024)
 
 
-def column_kernel(x_ref, c_ref, wi_ref, wm_ref, wo_ref, out_ref, grad_ref, wit, wmt, wot, wmh, h1_ref, h2_ref, d1_ref, d2_ref, s1_ref, grid_ref, g1, g2, g3):
+def column_kernel(x_ref, c_ref, wi_ref, wm_ref, wo_ref, out_hbm, grad_ref, wit, wmt, wot, wmh, h1_ref, h2_ref, d1_ref, d2_ref, s1_ref, grid_ref, g1, g2, g3, out_ref, sems):
     n = pl.program_id(0)
 
     @pl.when(n == 0)
@@ -96,8 +104,15 @@
 
     @pl.when(n == STEPS - 1)
     def _():
+        copies = [
+            pltpu.make_async_copy(out_ref.at[:, pl.ds(LANES * t, LANES)], out_hbm.at[:, pl.ds(LANES * t, LANES)], sems.at[t])
+            for t in range(TILES)
+        ]
         for t in range(TILES):
             out_ref[:, LANES * t : LANES * (t + 1)] = grid_ref[LANES * t : LANES * (t + 1), :].T
+            copies[t].start()
+        for copy in copies:
+            copy.wait()
         at = 0
         for g in (g1, g2, g3):
             rows = g.shape[0]
@@ -115,7 +130,7 @@
         grid=(STEPS,),
         in_specs=[block, block] + [pl.BlockSpec(w.shape, lambda n: (0, 0)) for w in (wi, wm, wo)],
         out_specs=[
-            pl.BlockSpec((NLON, WIDTH), lambda n: (0, 0)),
+            HBM,
             pl.BlockSpec((GRAD_ROWS * WAYS, LANES), lambda n: (0, 0)),
         ],
         out_shape=[
@@ -136,8 +151,10 @@
             pltpu.VMEM((FEATURES, HIDDEN), jnp.float32),
             pltpu.VMEM((HIDDEN, HIDDEN), jnp.float32),
             pltpu.VMEM((FEATURES, HIDDEN), jnp.float32),
+            pltpu.VMEM((NLON, WIDTH), jnp.bfloat16),
+            pltpu.SemaphoreType.DMA((TILES,)),
         ],
-        compiler_params=params(48),
+        compiler_params=params(60),
         name="columns",
     )(x, c, wi, wm, wo)
 
@@ -206,28 +223,51 @@
             out_specs=[block, block],
         ),
         out_shape=[table, table],
-        compiler_params=params(40),
+        compiler_params=params(60),
         name="legendre",
     )(wave_local, legendre)
 
 
-def pack_out(wide_ref, out_ref):
+def group_copies(src, dst, sems):
+    return [pltpu.make_async_copy(src.at[pl.ds(GROUP * k, GROUP)], dst.at[pl.ds(GROUP * k, GROUP)], sems.at[k]) for k in range(GROUPS)]
+
+
+def pack_out(wide_ref, chunk_ref, out_hbm, sems, pitch):
+    rows = chunk_ref.shape[1]
+
     def body(p, carry):
-        out_ref[p] = wide_ref[pl.ds(PITCH * p, ROWS), :].astype(jnp.bfloat16)
+        chunk_ref[p] = wide_ref[pl.ds(pitch * p, rows), :].astype(jnp.bfloat16)
         return carry
 
-    lax.fori_loop(0, WAYS, body, 0, unroll=4)
-
-
-def unpack_in(in_ref, wide_ref):
+    copies = group_copies(chunk_ref, out_hbm, sems)
+    for k, copy in enumerate(copies):
+        lax.fori_loop(GROUP * k, GROUP * (k + 1), body, 0, unroll=4)
+        copy.start()
+    for copy in copies:
+        copy.wait()
+
+
+def unpack_in(in_hbm, chunk_ref, wide_ref, sems, pitch, then=()):
+    rows = chunk_ref.shape[1]
+
     def body(p, carry):
-        wide_ref[pl.ds(PITCH * p, ROWS), :] = in_ref[p].astype(jnp.float32)
+        wide_ref[pl.ds(pitch * p, rows), :] = chunk_ref[p].astype(jnp.float32)
         return carry
 
-    lax.fori_loop(0, WAYS, body, 0, unroll=4)
-
-
-def forward_kernel(x_ref, table_ref, out_ref, wide_ref):
+    copies = group_copies(in_hbm, chunk_ref, sems)
+    for copy in (*copies, *then):
+        copy.start()
+    for k, copy in enumerate(copies):
+        copy.wait()
+        lax.fori_loop(GROUP * k, GROUP * (k + 1), body, 0, unroll=4)
+
+
+CHUNKS = pltpu.VMEM((WAYS, ROWS, LANES), jnp.bfloat16)
+LATE_CHUNKS = pltpu.VMEM((WAYS, LATE_ROWS, LANES), jnp.bfloat16)
+GROUP_SEMS = pltpu.SemaphoreType.DMA((GROUPS,))
+
+
+def forward_kernel(x_ref, table_ref, grad_ref, out_hbm, wide_ref, chunk_ref, sems):
     def body(k, carry):
         piece = mm(table_ref[pl.ds(pl.multiple_of(256 * k, 256), 256), :], x_ref[...])
         for h in range(2):
@@ -238,33 +278,54 @@
         return carry
 
     lax.fori_loop(0, SLOTS, body, 0)
-    pack_out(wide_ref, out_ref)
-
-
-def forward(x, table):
+    for k in range(2):
+        wide_ref[pl.ds(DATA_ROWS + k, WAYS, stride=PITCH), :] = jnp.zeros((WAYS, LANES), jnp.float32)
+    wide_ref[pl.ds(DATA_ROWS, WAYS, stride=PITCH), :BLOCK_ROWS] = grad_ref[...].T
+    pack_out(wide_ref, chunk_ref, out_hbm, sems, PITCH)
+
+
+def forward(x, table, grad):
     return pl.pallas_call(
         forward_kernel,
-        in_specs=[VMEM] * 2,
-        out_specs=VMEM,
+        in_specs=[VMEM] * 3,
+        out_specs=HBM,
         out_shape=jax.ShapeDtypeStruct((WAYS, ROWS, LANES), jnp.bfloat16),
-        scratch_shapes=[pltpu.VMEM((WAYS * PITCH, LANES), jnp.float32)],
+        scratch_shapes=[pltpu.VMEM((WAYS * PITCH, LANES), jnp.float32), CHUNKS, GROUP_SEMS],
         compiler_params=params(24),
         name="forward",
-    )(x, table)
-
-
-def spectral_kernel(m_ref, in_ref, at_hbm, inv_hbm, as_hbm, out_ref, wide_ref, x_ref, bank_ref, at_ref, inv_ref, as_ref, sems):
+    )(x, table, grad)
+
+
+def sum_blocks(wide_ref, sums_ref):
+    slab = wide_ref[pl.ds(DATA_ROWS, WAYS, stride=PITCH), :].astype(jnp.bfloat16)
+    block = lax.broadcasted_iota(jnp.int32, (BLOCKS, WAYS), 0)
+    source = lax.broadcasted_iota(jnp.int32, (BLOCKS, WAYS), 1)
+    lat = source >> 3
+    owner = ((source & 1) << 4) | ((lat & 1) << 3) | (((lat >> 2) & 1) << 2) | (((lat >> 1) & 1) << 1) | (lat >> 3)
+    sums = mm((owner == block).astype(jnp.bfloat16), slab)
+    half = BLOCKS // 2
+    lane = lax.broadcasted_iota(jnp.int32, (half, LANES), 1)
+    sums_ref[:half, :] = jnp.where(lane < 64, sums[:half], pltpu.roll(sums[half:], 64, 1))
+    row = lax.broadcasted_iota(jnp.int32, (LANES, LANES), 0)
+    col = lax.broadcasted_iota(jnp.int32, (LANES, LANES), 1)
+    rest = mm(sums.astype(jnp.bfloat16), (row == 64 + (col & 7)).astype(jnp.bfloat16))
+    keep = (lane >> 3) == lax.broadcasted_iota(jnp.int32, (half, LANES), 0)
+    for h in range(2):
+        part = jnp.where(keep, rest[half * h : half * (h + 1)], 0.0)
+        sums_ref[half + h : half + h + 1, :] = jnp.sum(part, axis=0, keepdims=True)
+
+
+def spectral_kernel(
+    m_ref, in_hbm, at_hbm, inv_hbm, as_hbm, out_hbm, wide_ref, chunk_ref, late_ref, x_ref, bank_ref, at_ref, inv_ref, as_ref, sums_ref, sems, group_sems
+):
     at_copy = pltpu.make_async_copy(at_hbm, at_ref, sems.at[0])
     inv_copies = []
     for k in range(INV_PARTS):
         part = pl.ds(k * (NDEG // INV_PARTS), NDEG // INV_PARTS)
         inv_copies.append(pltpu.make_async_copy(inv_hbm.at[part], inv_ref.at[part], sems.at[2 + k]))
     as_copy = pltpu.make_async_copy(as_hbm, as_ref, sems.at[1])
-    at_copy.start()
-    for copy in inv_copies:
-        copy.start()
-    as_copy.start()
-    unpack_in(in_ref, wide_ref)
+    unpack_in(in_hbm, chunk_ref, wide_ref, group_sems, PITCH, [at_copy, *inv_copies, as_copy])
+    sum_blocks(wide_ref, sums_ref)
     lane = lax.broadcasted_iota(jnp.int32, (WAYS, LANES), 1)
 
     def analyse(s, carry):
@@ -317,82 +378,96 @@
                 if off + LEVELS > LANES:
                     tiles[t + 1] = piece
             for t in range(TILES):
-                wide_ref[pl.ds((2 * s + r) * TILES + t, WAYS, stride=PITCH), :] = tiles[t]
+                wide_ref[pl.ds((2 * s + r) * TILES + t, WAYS, stride=LATE_PITCH), :] = tiles[t]
         return carry
 
     as_copy.wait()
     lax.fori_loop(0, SLOTS, synthesise, 0)
-    pack_out(wide_ref, out_ref)
+    for k in range(GRAD_ROWS):
+        row = jnp.broadcast_to(sums_ref[k : k + 1, :], (WAYS, LANES))
+        wide_ref[pl.ds(DATA_ROWS + k, WAYS, stride=LATE_PITCH), :] = row
+    pack_out(wide_ref, late_ref, out_hbm, group_sems, LATE_PITCH)
 
 
 def spectral(wave_local, arrived, at, inv, synth):
     return pl.pallas_call(
         spectral_kernel,
-        in_specs=[SMEM, VMEM, ANY, ANY, ANY],
-        out_specs=VMEM,
-        out_shape=jax.ShapeDtypeStruct((WAYS, ROWS, LANES), jnp.bfloat16),
+        in_specs=[SMEM, ANY, ANY, ANY, ANY],
+        out_specs=HBM,
+        out_shape=jax.ShapeDtypeStruct((WAYS, LATE_ROWS, LANES), jnp.bfloat16),
         scratch_shapes=[
-            pltpu.VMEM((WAYS * PITCH, LANES), jnp.float32),
+            pltpu.VMEM((WAYS * LATE_PITCH, LANES), jnp.float32),
+            CHUNKS,
+            LATE_CHUNKS,
             pltpu.VMEM((NLAT, 4 * LANES), jnp.bfloat16),
             pltpu.VMEM((NDEG * BANK, LANES), jnp.float32),
             pltpu.VMEM((SLOTS, NDEG, NLAT), jnp.bfloat16),
             pltpu.VMEM((NDEG, LEVELS, LEVELS), jnp.bfloat16),
             pltpu.VMEM((SLOTS, NLAT, NDEG), jnp.bfloat16),
+            pltpu.VMEM((24, LANES), jnp.float32),
             pltpu.SemaphoreType.DMA((2 + INV_PARTS,)),
+            GROUP_SEMS,
         ],
-        compiler_params=params(46),
+        compiler_params=params(60),
         name="spectral",
     )(wave_local, arrived, at, inv, synth)
 
 
-def inverse_kernel(in_ref, table_ref, out_ref, wide_ref, rows_ref):
-    unpack_in(in_ref, wide_ref)
+def inverse_kernel(in_hbm, table_ref, out_hbm, g1, g2, g3, wide_ref, chunk_ref, rows_ref, out_ref, grad_ref, group_sems, sems):
+    unpack_in(in_hbm, chunk_ref, wide_ref, group_sems, LATE_PITCH)
     for t in range(TILES):
         for c in range(2 * SLOTS):
-            slab = wide_ref[pl.ds(TILES * c + t, WAYS, stride=PITCH), :]
+            slab = wide_ref[pl.ds(TILES * c + t, WAYS, stride=LATE_PITCH), :]
             rows_ref[LANES * t : LANES * (t + 1), WAYS * c : WAYS * (c + 1)] = slab.T.astype(jnp.bfloat16)
+    copies = []
     for i in range(SLOTS):
         out_ref[i] = mm(rows_ref[FEATURES * i : FEATURES * (i + 1), :], table_ref[...])
-
-
-def inverse(arrived, table):
-    return pl.pallas_call(
-        inverse_kernel,
-        in_specs=[VMEM] * 2,
-        out_specs=VMEM,
-        out_shape=jax.ShapeDtypeStruct((SLOTS, FEATURES, NLON), jnp.float32),
-        scratch_shapes=[
-            pltpu.VMEM((WAYS * PITCH, LANES), jnp.float32),
-            pltpu.VMEM((WIDTH, NLON), jnp.bfloat16),
-        ],
-        compiler_params=params(28),
-        name="inverse",
-    )(arrived, table)
-
-
-def unstack_kernel(in_ref, g1, g2, g3):
+        copies.append(pltpu.make_async_copy(out_ref.at[i], out_hbm.at[i], sems.at[i]))
+        copies[i].start()
+    half = BLOCKS // 2
+    for k in range(half):
+        both = wide_ref[pl.ds(DATA_ROWS + k, WAYS, stride=LATE_PITCH), :].T
+        for h in range(2):
+            at = BLOCK_ROWS * (k + half * h)
+            grad_ref[at : at + 64, :] = both[64 * h : 64 * (h + 1), :]
+    for h in range(2):
+        rest = wide_ref[pl.ds(DATA_ROWS + half + h, WAYS, stride=LATE_PITCH), :].T
+        for k in range(half):
+            at = BLOCK_ROWS * (k + half * h) + 64
+            grad_ref[at : at + 8, :] = rest[8 * k : 8 * (k + 1), :]
     scale = 1.0 / math.sqrt(NLAT * NLON)
     at = 0
     for g in (g1, g2, g3):
         rows = g.shape[0]
         for t in range(HIDDEN // LANES):
-            g[:, LANES * t : LANES * (t + 1)] = in_ref[at : at + rows, :].astype(jnp.float32) * scale
+            g[:, LANES * t : LANES * (t + 1)] = grad_ref[at : at + rows, :] * scale
             at += rows
-
-
-def unstack(grad):
+    for copy in copies:
+        copy.wait()
+
+
+def inverse(arrived, table):
     return pl.pallas_call(
-        unstack_kernel,
-        in_specs=[VMEM],
-        out_specs=[VMEM] * 3,
-        out_shape=[jax.ShapeDtypeStruct((r, HIDDEN), jnp.float32) for r in (FEATURES, HIDDEN, FEATURES)],
-        compiler_params=params(8),
-        name="unstack",
-    )(grad)
-
-
-STAGES = (("lev", 1), ("lat", 1), ("lat", 4), ("lat", 2), ("lat", 8), ("lev", 2), ("lev", 4))
-EARLY = 4
+        inverse_kernel,
+        in_specs=[ANY, VMEM],
+        out_specs=[HBM, VMEM, VMEM, VMEM],
+        out_shape=[jax.ShapeDtypeStruct((SLOTS, FEATURES, NLON), jnp.float32)]
+        + [jax.ShapeDtypeStruct((r, HIDDEN), jnp.float32) for r in (FEATURES, HIDDEN, FEATURES)],
+        scratch_shapes=[
+            pltpu.VMEM((WAYS * LATE_PITCH, LANES), jnp.float32),
+            LATE_CHUNKS,
+            pltpu.VMEM((WIDTH, NLON), jnp.bfloat16),
+            pltpu.VMEM((SLOTS, FEATURES, NLON), jnp.float32),
+            pltpu.VMEM((GRAD_ROWS * WAYS, LANES), jnp.float32),
+            GROUP_SEMS,
+            pltpu.SemaphoreType.DMA((SLOTS,)),
+        ],
+        compiler_params=params(28),
+        name="inverse",
+    )(arrived, table)
+
+
+STAGES = (("lev", 1), ("lat", 1), ("lat", 4), ("lat", 2), ("lat", 8))
 
 
 def across(array, axis, bit):
@@ -412,10 +487,8 @@
     return jnp.where(mine, high, low) + across(sent, axis, bit).astype(jnp.float32)
 
 
-def double(part, axis, bit):
-    other = across(part, axis, bit)
-    mine = upper(axis, bit)
-    return jnp.concatenate([jnp.where(mine, other, part), jnp.where(mine, part, other)])
+def in_hbm(array):
+    return pltpu.with_memory_space_constraint(array, pltpu.HBM)
 
 
 def swap(array, axis):
@@ -423,29 +496,20 @@
 
 
 def program(x, c, wi, wm, wo, legendre, level_inverse, wave_order):
-    x, c, wi, wm, wo = (pltpu.with_memory_space_constraint(a, pltpu.HBM) for a in (x, c, wi, wm, wo))
-    grid, grad = columns(x, c, wi, wm, wo)
+    grid, grad = columns(*map(in_hbm, (x, c, wi, wm, wo)))
     grid, legendre, level_inverse, wave_order = lax.optimization_barrier((grid, legendre, level_inverse, wave_order))
     rows = swap(grid.reshape(8, LONB, WIDTH), "lev")
     rows = rows.reshape(NLON, WIDTH)
     wave_local = lax.dynamic_slice_in_dim(wave_order, lax.axis_index(EVERYWHERE) * SLOTS, SLOTS)
     table = wave_table(wave_order)
-    for axis, bit in STAGES[:EARLY]:
+    for axis, bit in STAGES:
         grad = halve(grad, axis, bit)
     rows, table, grad = lax.optimization_barrier((rows, table, grad))
     at, synth = legendre_tables(wave_local, legendre)
     inv = level_inverse.transpose(2, 0, 1)
-    arrived = swap(forward(rows, table), EVERYWHERE)
+    arrived = swap(forward(rows, table, grad), EVERYWHERE)
     zonal = spectral(wave_local, arrived, at, inv, synth)
-    zonal, grad = lax.optimization_barrier((zonal, grad))
-    for axis, bit in STAGES[EARLY:]:
-        grad = halve(grad, axis, bit)
-    grad = grad.astype(jnp.bfloat16)
-    for axis, bit in STAGES[::-1]:
-        grad = double(grad, axis, bit)
-    g1, g2, g3 = unstack(grad)
-    arrived = swap(zonal, EVERYWHERE)
-    out = inverse(arrived, table)
+    out, g1, g2, g3 = inverse(swap(zonal, EVERYWHERE), table)
     return g1, g2, g3, out.transpose(1, 0, 2)
 
 

time: 215 us -> 193 us (0.90)
  waiting for transfers between devices: 68.2 us -> 19.1 us
  blocking collectives: 0 us -> 44.8 us
  starting transfers between devices: 42.1 us -> 23.2 us
  local copies, waits for them, and re-layouts: 31.9 us -> 23.1 us
  Pallas kernels: 65.6 us -> 74.2 us
    ppermute x14 -> x5, waiting for transfers between devices: 57.7 us -> 5.21 us  [across(): return lax.ppermute(array, axis, [(i, i ^ bit) for i in range(size)])]
    all_to_all x0 -> x1, blocking collectives: none -> 44.8 us  [swap(): return lax.all_to_all(array, axis, split_axis=0, concat_axis=0, tiled=True)]
    all_to_all x3 -> x2, starting transfers between devices: 23.4 us -> 13.7 us  [swap(): return lax.all_to_all(array, axis, split_axis=0, concat_axis=0, tiled=True)]
    unnamed x22 -> x8, local copies, waits for them, and re-layouts: 12.7 us -> 3.34 us
    ppermute x14 -> x5, starting transfers between devices: 18.7 us -> 9.53 us  [across(): return lax.ppermute(array, axis, [(i, i ^ bit) for i in range(size)])]
    pallas_call x4 -> x3, Pallas kernels: 36.8 us -> 41.3 us  [the longest x1 27.5 us: spectral(): pl.pallas_call(spectral_kernel, in_specs=[SMEM, ANY, ANY, ANY, ANY], out_...]
    all_to_all x3 -> x2, waiting for transfers between devices: 10.5 us -> 13.9 us  [swap(): return lax.all_to_all(array, axis, split_axis=0, concat_axis=0, tiled=True)]
  transfers between devices with their start and end apart: 17 -> 7, of which waited for: 13 -> 5; matrix products, arithmetic and copies ran while one was open for 11% -> 12% of each run, Pallas kernels for 5% -> 6%
where the time goes in v3:
time: 193 us; the launch traced here: 192 us
  Pallas kernels  74.2 us (38%)
  blocking collectives  44.8 us (23%)
  starting transfers between devices  23.2 us (12%)
  local copies, waits for them, and re-layouts  23.1 us (12%)
  waiting for transfers between devices  19.1 us (10%)
  other arithmetic  6.21 us (3%)
    all_to_all x1, blocking collectives, swap(): return lax.all_to_all(array, axis, split_axis=0, concat_axis=0, tiled=True)  44.8 us
    pallas_call x1, Pallas kernels, spectral(): pl.pallas_call(spectral_kernel, in_specs=[SMEM, ANY, ANY, ANY, ANY], out_...  27.5 us
    pallas_call x1, Pallas kernels, columns(): pl.pallas_call(column_kernel, grid=(STEPS,), in_specs=[block, block] + [p...  21.3 us
    optimization_barrier x1, local copies, waits for them, and re-layouts, program(): lax.optimization_barrier((grid, legendre, level_inverse, wave_order))  18.7 us
    all_to_all x2, waiting for transfers between devices, swap(): return lax.all_to_all(array, axis, split_axis=0, concat_axis=0, tiled=True)  13.9 us
    all_to_all x2, starting transfers between devices, swap(): return lax.all_to_all(array, axis, split_axis=0, concat_axis=0, tiled=True)  13.7 us
    pallas_call x1, Pallas kernels, legendre_tables(): pl.pallas_call(legendre_kernel, grid_spec=pltpu.PrefetchScalarGridSpec(nu...  9.74 us
    ppermute x5, starting transfers between devices, across(): return lax.ppermute(array, axis, [(i, i ^ bit) for i in range(size)])  9.53 us
  transfers between devices with their start and end apart: 7, of which 5 were waited for; matrix products, arithmetic and copies ran while one was open for 12% of the time, Pallas kernels for 6%

profile of v3, /device:TPU:0, one launch (start us, length us, event | category | flops | bytes accessed | tf_op | source)
XLA Modules:
  0.0 191.5 jit_solution(16780103125386791778)
XLA Ops:
  0.6 21.3 %columns.1 = (bf16[1280,896]{1,0:T(8,128)(2,1)}, f32[2304,128]{1,0:T(8,128)}) custom-call(bf16[176,6400]{1,0:T(8,128)(2,1)} %x_ref.1, bf16[176,6400]{1,0:T(8,128)(2,1)} %c_ref.1, bf16[176,384]{1,0:T(8,128)(2,1)} %wi_ref.1, bf16[384,384]{1,0:T(8,128)(2,1)} %wm_ref.1, bf16[176,384]{1,0:T(8,128)(2,1)} %wo_ref.1), custom_call_target="tpu_custom_call" | custom-call | tf_op jit(solution)/shard_map/columns/pallas_call | solution.py:128
  22.0 1.3 select_convert_fusion
  23.4 1.6 collective-permute-done
  24.9 1.3 convert_add_fusion
  26.3 1.7 collective-permute-start.1
  28.0 5.3 %all-to-all-start = ((bf16[8,160,896]{2,1,0:T(8,128)(2,1)}), bf16[8,160,896]{2,1,0:T(8,128)(2,1)}, u32[]{:S(2)}, u32[]{:S(2)}) async-start(bf16[8,160,896]{2,1,0:T(8,128)(2,1)} %bitcast), calls=%async_computation | async-start | bytes 4587520 | tf_op jit(solution)/shard_map/all_to_all | solution.py:495
  33.7 1.7 collective-permute-start.2
  35.6 2.8 %collective-permute-done.2 = bf16[288,128]{1,0:T(8,128)(2,1)S(1)} collective-permute-done((bf16[288,128]{1,0:T(8,128)(2,1)S(1)}, bf16[288,128]{1,0:T(8,128)(2,1)S(1)}, u32[]{:S(2)}, u32[]{:S(2)}) %collective-permute-start.2) | collective-permute-done | bytes 73760 | tf_op jit(solution)/shard_map/ppermute | solution.py:475
  38.5 2.8 %collective-permute-start.3 = (bf16[144,128]{1,0:T(8,128)(2,1)S(1)}, bf16[144,128]{1,0:T(8,128)(2,1)S(1)}, u32[]{:S(2)}, u32[]{:S(2)}) collective-permute-start(bf16[144,128]{1,0:T(8,128)(2,1)S(1)} %select_convert_fusion.3), channel_id=1, source_target_pairs={{0,16},{8,24},{16,0},{24,8},{32,48},{40,56},{48,32},{56,40},{64,80... | collective-permute-start | bytes 110600 | tf_op jit(solution)/shard_map/ppermute | solution.py:475
  41.3 1.9 multiply_sine_fusion
  44.0 3.3 %collective-permute-start.4 = (bf16[72,128]{1,0:T(8,128)(2,1)S(1)}, bf16[72,128]{1,0:T(8,128)(2,1)S(1)}, u32[]{:S(2)}, u32[]{:S(2)}) collective-permute-start(bf16[72,128]{1,0:T(8,128)(2,1)S(1)} %select_convert_fusion.4), channel_id=1, source_target_pairs={{0,64},{8,72},{16,80},{24,88},{32,96},{40,104},{48,112},{56,120},{... | collective-permute-start | bytes 55304 | tf_op jit(solution)/shard_map/ppermute | solution.py:475
  47.3 1.4 sine_multiply_fusion
  49.7 1.0 copy-done.2
  50.7 1.8 waves.1.table_ref
  52.5 10.1 %all-to-all-done = bf16[8,160,896]{2,1,0:T(8,128)(2,1)} async-done(((bf16[8,160,896]{2,1,0:T(8,128)(2,1)}), bf16[8,160,896]{2,1,0:T(8,128)(2,1)}, u32[]{:S(2)}, u32[]{:S(2)}) %all-to-all-start) | async-done | bytes 2293792 | tf_op jit(solution)/shard_map/all_to_all | solution.py:495
  62.7 6.9 %forward.1 = bf16[128,72,128]{2,1,0:T(8,128)(2,1)S(1)} custom-call(bf16[1280,896]{1,0:T(8,128)(2,1)} %bitcast.1.x_ref, bf16[1280,1280]{1,0:T(8,128)(2,1)S(1)} %waves.1.table_ref, f32[72,128]{1,0:T(8,128)S(1)} %convert_add_fusion.4.grad_ref), custom_call_target="tpu_custom_call" | custom-call | tf_op jit(solution)/shard_map/forward/pallas_call | solution.py:288
  69.6 1.4 copy-done
  71.0 8.4 %all-to-all-start.1 = ((bf16[128,72,128]{2,1,0:T(8,128)(2,1)}), bf16[128,72,128]{2,1,0:T(8,128)(2,1)}, u32[]{:S(2)}, u32[]{:S(2)}) async-start(bf16[128,72,128]{2,1,0:T(8,128)(2,1)} %copy-done), calls=%async_computation.1 | async-start | bytes 4718592 | tf_op jit(solution)/shard_map/all_to_all | solution.py:495
  80.0 18.7 %copy.17 = bf16[88,88,640]{1,0,2:T(8,128)(2,1)} copy(bf16[88,88,640]{2,1,0:T(8,128)(2,1)} %param.14) | data formatting | bytes 19824640 | tf_op jit(solution)/shard_map/optimization_barrier | solution.py:500
  98.7 9.7 %legendre.1 = (bf16[5,640,640]{2,1,0:T(8,128)(2,1)}, bf16[5,640,640]{2,1,0:T(8,128)(2,1)}) custom-call(s32[5]{0:T(128)} %dynamic_slice.3.m_ref, bf16[5,320,640]{2,1,0:T(8,128)(2,1)} %leg_ref), custom_call_target="tpu_custom_call" | custom-call | tf_op jit(solution)/shard_map/legendre/pallas_call | solution.py:217
  108.4 3.8 %all-to-all-done.1.in_hbm = bf16[128,72,128]{2,1,0:T(8,128)(2,1)} async-done(((bf16[128,72,128]{2,1,0:T(8,128)(2,1)}), bf16[128,72,128]{2,1,0:T(8,128)(2,1)}, u32[]{:S(2)}, u32[]{:S(2)}) %all-to-all-start.1) | async-done | bytes 2359328 | tf_op jit(solution)/shard_map/all_to_all | solution.py:495
  112.2 27.5 %spectral.1 = bf16[128,88,128]{2,1,0:T(8,128)(2,1)} custom-call(s32[5]{0:T(128)} %dynamic_slice.3.m_ref, bf16[128,72,128]{2,1,0:T(8,128)(2,1)} %all-to-all-done.1.in_hbm, bf16[5,640,640]{2,1,0:T(8,128)(2,1)} %get-tuple-element.27.at_hbm, bf16[640,88,88]{2,1,0:T(8,128)(2,1)} %bitcast.6, bf16[5,640,640]{2,1,0:T(8,128)(2,1)} %get-tuple-element.29.as_hbm), custom_call_target="tpu_custom_call" | custom-call | tf_op jit(solution)/shard_map/spectral/pallas_call | solution.py:393
  139.7 44.8 %all_to_all.15.in_hbm = bf16[128,88,128]{2,1,0:T(8,128)(2,1)S(1)} all-to-all(bf16[128,88,128]{2,1,0:T(8,128)(2,1)} %spectral.1), channel_id=1, replica_groups=mesh['lat'=16,'lev'=8] {'lat','lev'}, dimensions={0} | all-to-all | bytes 5767168 | tf_op jit(solution)/shard_map/all_to_all | solution.py:495
  184.5 6.9 %inverse.1 = (f32[5,176,1280]{2,1,0:T(8,128)}, f32[176,384]{1,0:T(8,128)}, f32[384,384]{1,0:T(8,128)}, f32[176,384]{1,0:T(8,128)}) custom-call(bf16[128,88,128]{2,1,0:T(8,128)(2,1)S(1)} %all_to_all.15.in_hbm, bf16[1280,1280]{1,0:T(8,128)(2,1)S(1)} %waves.1.table_ref), custom_call_target="tpu_custom_call" | custom-call | tf_op jit(solution)/shard_map/inverse/pallas_call | solution.py:450
  (24 shorter events, 3.2 us)
Async XLA Ops:
  23.3 1.7 collective-permute-start
  26.3 7.0 %copy-start.3 = (s32[640]{0:T(1024)S(1)}, s32[640]{0:T(1024)}, u32[]{:S(2)}) copy-start(s32[640]{0:T(1024)} %param.15) | copy-start | bytes 7684
  26.3 7.3 %collective-permute-start.1 = (bf16[576,128]{1,0:T(8,128)(2,1)S(1)}, bf16[576,128]{1,0:T(8,128)(2,1)S(1)}, u32[]{:S(2)}, u32[]{:S(2)}) collective-permute-start(bf16[576,128]{1,0:T(8,128)(2,1)S(1)} %select_convert_fusion.1), channel_id=1, source_target_pairs={{0,8},{8,0},{16,24},{24,16},{32,40},{40,32},{48,56},{56,48},{64,72... | collective-permute-start | bytes 442376 | tf_op jit(solution)/shard_map/ppermute | solution.py:475
  28.0 34.7 %all-to-all-start = ((bf16[8,160,896]{2,1,0:T(8,128)(2,1)}), bf16[8,160,896]{2,1,0:T(8,128)(2,1)}, u32[]{:S(2)}, u32[]{:S(2)}) async-start(bf16[8,160,896]{2,1,0:T(8,128)(2,1)} %bitcast), calls=%async_computation | async-start | bytes 4587520 | tf_op jit(solution)/shard_map/all_to_all | solution.py:495
  33.7 4.8 %collective-permute-start.2 = (bf16[288,128]{1,0:T(8,128)(2,1)S(1)}, bf16[288,128]{1,0:T(8,128)(2,1)S(1)}, u32[]{:S(2)}, u32[]{:S(2)}) collective-permute-start(bf16[288,128]{1,0:T(8,128)(2,1)S(1)} %select_convert_fusion.2), channel_id=1, source_target_pairs={{0,32},{8,40},{16,48},{24,56},{32,0},{40,8},{48,16},{56,24},{64,96... | collective-permute-start | bytes 221192 | tf_op jit(solution)/shard_map/ppermute | solution.py:475
  38.5 5.5 %collective-permute-start.3 = (bf16[144,128]{1,0:T(8,128)(2,1)S(1)}, bf16[144,128]{1,0:T(8,128)(2,1)S(1)}, u32[]{:S(2)}, u32[]{:S(2)}) collective-permute-start(bf16[144,128]{1,0:T(8,128)(2,1)S(1)} %select_convert_fusion.3), channel_id=1, source_target_pairs={{0,16},{8,24},{16,0},{24,8},{32,48},{40,56},{48,32},{56,40},{64,80... | collective-permute-start | bytes 110600 | tf_op jit(solution)/shard_map/ppermute | solution.py:475
  44.0 8.5 %collective-permute-start.4 = (bf16[72,128]{1,0:T(8,128)(2,1)S(1)}, bf16[72,128]{1,0:T(8,128)(2,1)S(1)}, u32[]{:S(2)}, u32[]{:S(2)}) collective-permute-start(bf16[72,128]{1,0:T(8,128)(2,1)S(1)} %select_convert_fusion.4), channel_id=1, source_target_pairs={{0,64},{8,72},{16,80},{24,88},{32,96},{40,104},{48,112},{56,120},{... | collective-permute-start | bytes 55304 | tf_op jit(solution)/shard_map/ppermute | solution.py:475
  48.7 1.0 copy-start.1
  49.7 1.0 copy-start.2
  69.6 1.4 copy-start
  71.0 41.2 %all-to-all-start.1 = ((bf16[128,72,128]{2,1,0:T(8,128)(2,1)}), bf16[128,72,128]{2,1,0:T(8,128)(2,1)}, u32[]{:S(2)}, u32[]{:S(2)}) async-start(bf16[128,72,128]{2,1,0:T(8,128)(2,1)} %copy-done), calls=%async_computation.1 | async-start | bytes 4718592 | tf_op jit(solution)/shard_map/all_to_all | solution.py:495

commit v4 on v3

--- a/solution.py
+++ b/solution.py
@@ -32,6 +32,7 @@
 STEPS = COLS // NLON
 BANK = 25
 INV_PARTS = 5
+AHEAD = 3
 PITCH = 73
 LATE_PITCH = 89
 EVERYWHERE = ("lat", "lev")
@@ -111,8 +112,6 @@
         for t in range(TILES):
             out_ref[:, LANES * t : LANES * (t + 1)] = grid_ref[LANES * t : LANES * (t + 1), :].T
             copies[t].start()
-        for copy in copies:
-            copy.wait()
         at = 0
         for g in (g1, g2, g3):
             rows = g.shape[0]
@@ -120,6 +119,8 @@
                 grad_ref[at : at + rows, :] = g[:, LANES * t : LANES * (t + 1)]
                 at += rows
         grad_ref[at:, :] = jnp.zeros((GRAD_ROWS * WAYS - at, LANES), jnp.float32)
+        for copy in copies:
+            copy.wait()
 
 
 def columns(x, c, wi, wm, wo):
@@ -324,7 +325,10 @@
         part = pl.ds(k * (NDEG // INV_PARTS), NDEG // INV_PARTS)
         inv_copies.append(pltpu.make_async_copy(inv_hbm.at[part], inv_ref.at[part], sems.at[2 + k]))
     as_copy = pltpu.make_async_copy(as_hbm, as_ref, sems.at[1])
-    unpack_in(in_hbm, chunk_ref, wide_ref, group_sems, PITCH, [at_copy, *inv_copies, as_copy])
+    at_copy.start()
+    unpack_in(in_hbm, chunk_ref, wide_ref, group_sems, PITCH)
+    for copy in inv_copies[:AHEAD]:
+        copy.start()
     sum_blocks(wide_ref, sums_ref)
     lane = lax.broadcasted_iota(jnp.int32, (WAYS, LANES), 1)
 
@@ -355,6 +359,8 @@
             bank_ref[rows, :LEVELS] = mm(bank_ref[rows, :LEVELS].astype(jnp.bfloat16), inv_ref[deg])
         return carry
 
+    for copy in (*inv_copies[AHEAD:], as_copy):
+        copy.start()
     steps = NDEG // 16 // INV_PARTS
     for k, copy in enumerate(inv_copies):
         copy.wait()

time: 193 us -> 188 us (0.974)
  Pallas kernels: 74.2 us -> 70 us
    pallas_call x1, Pallas kernels: 27.5 us -> 23.4 us  [spectral(): pl.pallas_call(spectral_kernel, in_specs=[SMEM, ANY, ANY, ANY, ANY], out_...]
where the time goes in v4:
time: 188 us; the launch traced here: 187 us
  Pallas kernels  70 us (37%)
  blocking collectives  44.8 us (24%)
  starting transfers between devices  23.2 us (12%)
  local copies, waits for them, and re-layouts  23.1 us (12%)
  waiting for transfers between devices  19.1 us (10%)
  other arithmetic  6.21 us (3%)
    all_to_all x1, blocking collectives, swap(): return lax.all_to_all(array, axis, split_axis=0, concat_axis=0, tiled=True)  44.8 us
    pallas_call x1, Pallas kernels, spectral(): pl.pallas_call(spectral_kernel, in_specs=[SMEM, ANY, ANY, ANY, ANY], out_...  23.4 us
    pallas_call x1, Pallas kernels, columns(): pl.pallas_call(column_kernel, grid=(STEPS,), in_specs=[block, block] + [p...  21.2 us
    optimization_barrier x1, local copies, waits for them, and re-layouts, program(): lax.optimization_barrier((grid, legendre, level_inverse, wave_order))  18.7 us
    all_to_all x2, waiting for transfers between devices, swap(): return lax.all_to_all(array, axis, split_axis=0, concat_axis=0, tiled=True)  13.9 us
    all_to_all x2, starting transfers between devices, swap(): return lax.all_to_all(array, axis, split_axis=0, concat_axis=0, tiled=True)  13.7 us
    pallas_call x1, Pallas kernels, legendre_tables(): pl.pallas_call(legendre_kernel, grid_spec=pltpu.PrefetchScalarGridSpec(nu...  9.74 us
    ppermute x5, starting transfers between devices, across(): return lax.ppermute(array, axis, [(i, i ^ bit) for i in range(size)])  9.53 us
  transfers between devices with their start and end apart: 7, of which 5 were waited for; matrix products, arithmetic and copies ran while one was open for 12% of the time, Pallas kernels for 6%

profile of v4, /device:TPU:0, one launch (start us, length us, event | category | flops | bytes accessed | tf_op | source)
XLA Modules:
  0.0 187.3 jit_solution(11329524380549106075)
XLA Ops:
  0.6 21.2 %columns.1 = (bf16[1280,896]{1,0:T(8,128)(2,1)}, f32[2304,128]{1,0:T(8,128)}) custom-call(bf16[176,6400]{1,0:T(8,128)(2,1)} %x_ref.1, bf16[176,6400]{1,0:T(8,128)(2,1)} %c_ref.1, bf16[176,384]{1,0:T(8,128)(2,1)} %wi_ref.1, bf16[384,384]{1,0:T(8,128)(2,1)} %wm_ref.1, bf16[176,384]{1,0:T(8,128)(2,1)} %wo_ref.1), custom_call_target="tpu_custom_call" | custom-call | tf_op jit(solution)/shard_map/columns/pallas_call | solution.py:129
  21.9 1.3 select_convert_fusion
  23.3 1.6 collective-permute-done
  24.8 1.3 convert_add_fusion
  26.2 1.7 collective-permute-start.1
  27.9 5.3 %all-to-all-start = ((bf16[8,160,896]{2,1,0:T(8,128)(2,1)}), bf16[8,160,896]{2,1,0:T(8,128)(2,1)}, u32[]{:S(2)}, u32[]{:S(2)}) async-start(bf16[8,160,896]{2,1,0:T(8,128)(2,1)} %bitcast), calls=%async_computation | async-start | bytes 4587520 | tf_op jit(solution)/shard_map/all_to_all | solution.py:501
  33.6 1.7 collective-permute-start.2
  35.5 2.8 %collective-permute-done.2 = bf16[288,128]{1,0:T(8,128)(2,1)S(1)} collective-permute-done((bf16[288,128]{1,0:T(8,128)(2,1)S(1)}, bf16[288,128]{1,0:T(8,128)(2,1)S(1)}, u32[]{:S(2)}, u32[]{:S(2)}) %collective-permute-start.2) | collective-permute-done | bytes 73760 | tf_op jit(solution)/shard_map/ppermute | solution.py:481
  38.4 2.8 %collective-permute-start.3 = (bf16[144,128]{1,0:T(8,128)(2,1)S(1)}, bf16[144,128]{1,0:T(8,128)(2,1)S(1)}, u32[]{:S(2)}, u32[]{:S(2)}) collective-permute-start(bf16[144,128]{1,0:T(8,128)(2,1)S(1)} %select_convert_fusion.3), channel_id=1, source_target_pairs={{0,16},{8,24},{16,0},{24,8},{32,48},{40,56},{48,32},{56,40},{64,80... | collective-permute-start | bytes 110600 | tf_op jit(solution)/shard_map/ppermute | solution.py:481
  41.2 1.9 %multiply_sine_fusion = (f32[640,10]{1,0:T(8,128)}, f32[640,10]{1,0:T(8,128)}) fusion(f32[640,10]{1,0:T(8,128)S(1)} %copy.16), kind=kLoop, calls=%fused_computation.11 | loop fusion | flops 6400 | bytes 76800 | tf_op jit(solution)/shard_map/sin | solution.py:187
  44.0 3.3 %collective-permute-start.4 = (bf16[72,128]{1,0:T(8,128)(2,1)S(1)}, bf16[72,128]{1,0:T(8,128)(2,1)S(1)}, u32[]{:S(2)}, u32[]{:S(2)}) collective-permute-start(bf16[72,128]{1,0:T(8,128)(2,1)S(1)} %select_convert_fusion.4), channel_id=1, source_target_pairs={{0,64},{8,72},{16,80},{24,88},{32,96},{40,104},{48,112},{56,120},{... | collective-permute-start | bytes 55304 | tf_op jit(solution)/shard_map/ppermute | solution.py:481
  47.2 1.4 sine_multiply_fusion
  49.6 1.0 copy-done.2
  50.6 1.8 waves.1.table_ref
  52.5 10.1 %all-to-all-done = bf16[8,160,896]{2,1,0:T(8,128)(2,1)} async-done(((bf16[8,160,896]{2,1,0:T(8,128)(2,1)}), bf16[8,160,896]{2,1,0:T(8,128)(2,1)}, u32[]{:S(2)}, u32[]{:S(2)}) %all-to-all-start) | async-done | bytes 2293792 | tf_op jit(solution)/shard_map/all_to_all | solution.py:501
  62.6 6.9 %forward.1 = bf16[128,72,128]{2,1,0:T(8,128)(2,1)S(1)} custom-call(bf16[1280,896]{1,0:T(8,128)(2,1)} %bitcast.1.x_ref, bf16[1280,1280]{1,0:T(8,128)(2,1)S(1)} %waves.1.table_ref, f32[72,128]{1,0:T(8,128)S(1)} %convert_add_fusion.4.grad_ref), custom_call_target="tpu_custom_call" | custom-call | tf_op jit(solution)/shard_map/forward/pallas_call | solution.py:289
  69.5 1.4 copy-done
  70.9 8.4 %all-to-all-start.1 = ((bf16[128,72,128]{2,1,0:T(8,128)(2,1)}), bf16[128,72,128]{2,1,0:T(8,128)(2,1)}, u32[]{:S(2)}, u32[]{:S(2)}) async-start(bf16[128,72,128]{2,1,0:T(8,128)(2,1)} %copy-done), calls=%async_computation.1 | async-start | bytes 4718592 | tf_op jit(solution)/shard_map/all_to_all | solution.py:501
  79.9 18.7 %copy.17 = bf16[88,88,640]{1,0,2:T(8,128)(2,1)} copy(bf16[88,88,640]{2,1,0:T(8,128)(2,1)} %param.14) | data formatting | bytes 19824640 | tf_op jit(solution)/shard_map/optimization_barrier | solution.py:506
  98.6 9.7 %legendre.1 = (bf16[5,640,640]{2,1,0:T(8,128)(2,1)}, bf16[5,640,640]{2,1,0:T(8,128)(2,1)}) custom-call(s32[5]{0:T(128)} %dynamic_slice.3.m_ref, bf16[5,320,640]{2,1,0:T(8,128)(2,1)} %leg_ref), custom_call_target="tpu_custom_call" | custom-call | tf_op jit(solution)/shard_map/legendre/pallas_call | solution.py:218
  108.4 3.8 %all-to-all-done.1.in_hbm = bf16[128,72,128]{2,1,0:T(8,128)(2,1)} async-done(((bf16[128,72,128]{2,1,0:T(8,128)(2,1)}), bf16[128,72,128]{2,1,0:T(8,128)(2,1)}, u32[]{:S(2)}, u32[]{:S(2)}) %all-to-all-start.1) | async-done | bytes 2359328 | tf_op jit(solution)/shard_map/all_to_all | solution.py:501
  112.1 23.4 %spectral.1 = bf16[128,88,128]{2,1,0:T(8,128)(2,1)} custom-call(s32[5]{0:T(128)} %dynamic_slice.3.m_ref, bf16[128,72,128]{2,1,0:T(8,128)(2,1)} %all-to-all-done.1.in_hbm, bf16[5,640,640]{2,1,0:T(8,128)(2,1)} %get-tuple-element.27.at_hbm, bf16[640,88,88]{2,1,0:T(8,128)(2,1)} %bitcast.6, bf16[5,640,640]{2,1,0:T(8,128)(2,1)} %get-tuple-element.29.as_hbm), custom_call_target="tpu_custom_call" | custom-call | tf_op jit(solution)/shard_map/spectral/pallas_call | solution.py:399
  135.5 44.8 %all_to_all.15.in_hbm = bf16[128,88,128]{2,1,0:T(8,128)(2,1)S(1)} all-to-all(bf16[128,88,128]{2,1,0:T(8,128)(2,1)} %spectral.1), channel_id=1, replica_groups=mesh['lat'=16,'lev'=8] {'lat','lev'}, dimensions={0} | all-to-all | bytes 5767168 | tf_op jit(solution)/shard_map/all_to_all | solution.py:501
  180.3 6.9 %inverse.1 = (f32[5,176,1280]{2,1,0:T(8,128)}, f32[176,384]{1,0:T(8,128)}, f32[384,384]{1,0:T(8,128)}, f32[176,384]{1,0:T(8,128)}) custom-call(bf16[128,88,128]{2,1,0:T(8,128)(2,1)S(1)} %all_to_all.15.in_hbm, bf16[1280,1280]{1,0:T(8,128)(2,1)S(1)} %waves.1.table_ref), custom_call_target="tpu_custom_call" | custom-call | tf_op jit(solution)/shard_map/inverse/pallas_call | solution.py:456
  (24 shorter events, 3.2 us)
Async XLA Ops:
  23.2 1.7 collective-permute-start
  26.2 7.0 %copy-start.3 = (s32[640]{0:T(1024)S(1)}, s32[640]{0:T(1024)}, u32[]{:S(2)}) copy-start(s32[640]{0:T(1024)} %param.15) | copy-start | bytes 7684
  26.2 7.3 %collective-permute-start.1 = (bf16[576,128]{1,0:T(8,128)(2,1)S(1)}, bf16[576,128]{1,0:T(8,128)(2,1)S(1)}, u32[]{:S(2)}, u32[]{:S(2)}) collective-permute-start(bf16[576,128]{1,0:T(8,128)(2,1)S(1)} %select_convert_fusion.1), channel_id=1, source_target_pairs={{0,8},{8,0},{16,24},{24,16},{32,40},{40,32},{48,56},{56,48},{64,72... | collective-permute-start | bytes 442376 | tf_op jit(solution)/shard_map/ppermute | solution.py:481
  27.9 34.7 %all-to-all-start = ((bf16[8,160,896]{2,1,0:T(8,128)(2,1)}), bf16[8,160,896]{2,1,0:T(8,128)(2,1)}, u32[]{:S(2)}, u32[]{:S(2)}) async-start(bf16[8,160,896]{2,1,0:T(8,128)(2,1)} %bitcast), calls=%async_computation | async-start | bytes 4587520 | tf_op jit(solution)/shard_map/all_to_all | solution.py:501
  33.6 4.8 %collective-permute-start.2 = (bf16[288,128]{1,0:T(8,128)(2,1)S(1)}, bf16[288,128]{1,0:T(8,128)(2,1)S(1)}, u32[]{:S(2)}, u32[]{:S(2)}) collective-permute-start(bf16[288,128]{1,0:T(8,128)(2,1)S(1)} %select_convert_fusion.2), channel_id=1, source_target_pairs={{0,32},{8,40},{16,48},{24,56},{32,0},{40,8},{48,16},{56,24},{64,96... | collective-permute-start | bytes 221192 | tf_op jit(solution)/shard_map/ppermute | solution.py:481
  38.4 5.5 %collective-permute-start.3 = (bf16[144,128]{1,0:T(8,128)(2,1)S(1)}, bf16[144,128]{1,0:T(8,128)(2,1)S(1)}, u32[]{:S(2)}, u32[]{:S(2)}) collective-permute-start(bf16[144,128]{1,0:T(8,128)(2,1)S(1)} %select_convert_fusion.3), channel_id=1, source_target_pairs={{0,16},{8,24},{16,0},{24,8},{32,48},{40,56},{48,32},{56,40},{64,80... | collective-permute-start | bytes 110600 | tf_op jit(solution)/shard_map/ppermute | solution.py:481
  44.0 8.5 %collective-permute-start.4 = (bf16[72,128]{1,0:T(8,128)(2,1)S(1)}, bf16[72,128]{1,0:T(8,128)(2,1)S(1)}, u32[]{:S(2)}, u32[]{:S(2)}) collective-permute-start(bf16[72,128]{1,0:T(8,128)(2,1)S(1)} %select_convert_fusion.4), channel_id=1, source_target_pairs={{0,64},{8,72},{16,80},{24,88},{32,96},{40,104},{48,112},{56,120},{... | collective-permute-start | bytes 55304 | tf_op jit(solution)/shard_map/ppermute | solution.py:481
  48.7 1.0 copy-start.1
  49.6 1.0 copy-start.2
  69.5 1.4 copy-start
  70.9 41.2 %all-to-all-start.1 = ((bf16[128,72,128]{2,1,0:T(8,128)(2,1)}), bf16[128,72,128]{2,1,0:T(8,128)(2,1)}, u32[]{:S(2)}, u32[]{:S(2)}) async-start(bf16[128,72,128]{2,1,0:T(8,128)(2,1)} %copy-done), calls=%async_computation.1 | async-start | bytes 4718592 | tf_op jit(solution)/shard_map/all_to_all | solution.py:501

commit v5 on v4

--- a/solution.py
+++ b/solution.py
@@ -61,7 +61,7 @@
     return pltpu.CompilerParams(vmem_limit_bytes=mib * 1024 * 1024)
 
 
-def column_kernel(x_ref, c_ref, wi_ref, wm_ref, wo_ref, out_hbm, grad_ref, wit, wmt, wot, wmh, h1_ref, h2_ref, d1_ref, d2_ref, s1_ref, grid_ref, g1, g2, g3, out_ref, sems):
+def column_kernel(x_ref, c_ref, wi_ref, wm_ref, wo_ref, out_hbm, grad_hbm, wit, wmt, wot, wmh, h1_ref, h2_ref, d1_ref, d2_ref, s1_ref, grid_ref, g1, g2, g3, out_ref, grad_ref, sems):
     n = pl.program_id(0)
 
     @pl.when(n == 0)
@@ -109,9 +109,6 @@
             pltpu.make_async_copy(out_ref.at[:, pl.ds(LANES * t, LANES)], out_hbm.at[:, pl.ds(LANES * t, LANES)], sems.at[t])
             for t in range(TILES)
         ]
-        for t in range(TILES):
-            out_ref[:, LANES * t : LANES * (t + 1)] = grid_ref[LANES * t : LANES * (t + 1), :].T
-            copies[t].start()
         at = 0
         for g in (g1, g2, g3):
             rows = g.shape[0]
@@ -119,6 +116,12 @@
                 grad_ref[at : at + rows, :] = g[:, LANES * t : LANES * (t + 1)]
                 at += rows
         grad_ref[at:, :] = jnp.zeros((GRAD_ROWS * WAYS - at, LANES), jnp.float32)
+        grad_copy = pltpu.make_async_copy(grad_ref, grad_hbm, sems.at[TILES])
+        grad_copy.start()
+        for t in range(TILES):
+            out_ref[:, LANES * t : LANES * (t + 1)] = grid_ref[LANES * t : LANES * (t + 1), :].T
+            copies[t].start()
+        grad_copy.wait()
         for copy in copies:
             copy.wait()
 
@@ -132,7 +135,7 @@
         in_specs=[block, block] + [pl.BlockSpec(w.shape, lambda n: (0, 0)) for w in (wi, wm, wo)],
         out_specs=[
             HBM,
-            pl.BlockSpec((GRAD_ROWS * WAYS, LANES), lambda n: (0, 0)),
+            HBM,
         ],
         out_shape=[
             jax.ShapeDtypeStruct((NLON, WIDTH), jnp.bfloat16),
@@ -153,7 +156,8 @@
             pltpu.VMEM((HIDDEN, HIDDEN), jnp.float32),
             pltpu.VMEM((FEATURES, HIDDEN), jnp.float32),
             pltpu.VMEM((NLON, WIDTH), jnp.bfloat16),
-            pltpu.SemaphoreType.DMA((TILES,)),
+            pltpu.VMEM((GRAD_ROWS * WAYS, LANES), jnp.float32),
+            pltpu.SemaphoreType.DMA((TILES + 1,)),
         ],
         compiler_params=params(60),
         name="columns",
@@ -424,7 +428,7 @@
     for t in range(TILES):
         for c in range(2 * SLOTS):
             slab = wide_ref[pl.ds(TILES * c + t, WAYS, stride=LATE_PITCH), :]
-            rows_ref[LANES * t : LANES * (t + 1), WAYS * c : WAYS * (c + 1)] = slab.T.astype(jnp.bfloat16)
+            rows_ref[LANES * t : LANES * (t + 1), WAYS * c : WAYS * (c + 1)] = slab.astype(jnp.bfloat16).T
     copies = []
     for i in range(SLOTS):
         out_ref[i] = mm(rows_ref[FEATURES * i : FEATURES * (i + 1), :], table_ref[...])

time: 188 us -> 188 us (level)
  no operation moved by 1% of the time
where the time goes in v5:
time: 188 us; the launch traced here: 187 us
  Pallas kernels  69.3 us (37%)
  blocking collectives  44.8 us (24%)
  starting transfers between devices  23.2 us (12%)
  local copies, waits for them, and re-layouts  23.1 us (12%)
  waiting for transfers between devices  19.1 us (10%)
  other arithmetic  6.21 us (3%)
    all_to_all x1, blocking collectives, swap(): return lax.all_to_all(array, axis, split_axis=0, concat_axis=0, tiled=True)  44.8 us
    pallas_call x1, Pallas kernels, spectral(): pl.pallas_call(spectral_kernel, in_specs=[SMEM, ANY, ANY, ANY, ANY], out_...  23.4 us
    pallas_call x1, Pallas kernels, columns(): pl.pallas_call(column_kernel, grid=(STEPS,), in_specs=[block, block] + [p...  20.6 us
    optimization_barrier x1, local copies, waits for them, and re-layouts, program(): lax.optimization_barrier((grid, legendre, level_inverse, wave_order))  18.7 us
    all_to_all x2, waiting for transfers between devices, swap(): return lax.all_to_all(array, axis, split_axis=0, concat_axis=0, tiled=True)  13.9 us
    all_to_all x2, starting transfers between devices, swap(): return lax.all_to_all(array, axis, split_axis=0, concat_axis=0, tiled=True)  13.7 us
    pallas_call x1, Pallas kernels, legendre_tables(): pl.pallas_call(legendre_kernel, grid_spec=pltpu.PrefetchScalarGridSpec(nu...  9.74 us
    ppermute x5, starting transfers between devices, across(): return lax.ppermute(array, axis, [(i, i ^ bit) for i in range(size)])  9.52 us
  transfers between devices with their start and end apart: 7, of which 5 were waited for; matrix products, arithmetic and copies ran while one was open for 12% of the time, Pallas kernels for 6%

profile of v5, /device:TPU:0, one launch (start us, length us, event | category | flops | bytes accessed | tf_op | source)
XLA Modules:
  0.0 186.7 jit_solution(160383615726375203)
XLA Ops:
  0.6 20.6 %columns.1 = (bf16[1280,896]{1,0:T(8,128)(2,1)}, f32[2304,128]{1,0:T(8,128)}) custom-call(bf16[176,6400]{1,0:T(8,128)(2,1)} %x_ref.1, bf16[176,6400]{1,0:T(8,128)(2,1)} %c_ref.1, bf16[176,384]{1,0:T(8,128)(2,1)} %wi_ref.1, bf16[384,384]{1,0:T(8,128)(2,1)} %wm_ref.1, bf16[176,384]{1,0:T(8,128)(2,1)} %wo_ref.1), custom_call_target="tpu_custom_call" | custom-call | tf_op jit(solution)/shard_map/columns/pallas_call | solution.py:132
  21.2 1.3 select_convert_fusion
  22.6 1.6 collective-permute-done
  24.2 1.3 convert_add_fusion
  25.6 1.7 collective-permute-start.1
  27.3 5.3 %all-to-all-start = ((bf16[8,160,896]{2,1,0:T(8,128)(2,1)}), bf16[8,160,896]{2,1,0:T(8,128)(2,1)}, u32[]{:S(2)}, u32[]{:S(2)}) async-start(bf16[8,160,896]{2,1,0:T(8,128)(2,1)} %bitcast), calls=%async_computation | async-start | bytes 4587520 | tf_op jit(solution)/shard_map/all_to_all | solution.py:505
  32.9 1.7 collective-permute-start.2
  34.9 2.8 %collective-permute-done.2 = bf16[288,128]{1,0:T(8,128)(2,1)S(1)} collective-permute-done((bf16[288,128]{1,0:T(8,128)(2,1)S(1)}, bf16[288,128]{1,0:T(8,128)(2,1)S(1)}, u32[]{:S(2)}, u32[]{:S(2)}) %collective-permute-start.2) | collective-permute-done | bytes 73760 | tf_op jit(solution)/shard_map/ppermute | solution.py:485
  37.7 2.8 %collective-permute-start.3 = (bf16[144,128]{1,0:T(8,128)(2,1)S(1)}, bf16[144,128]{1,0:T(8,128)(2,1)S(1)}, u32[]{:S(2)}, u32[]{:S(2)}) collective-permute-start(bf16[144,128]{1,0:T(8,128)(2,1)S(1)} %select_convert_fusion.3), channel_id=1, source_target_pairs={{0,16},{8,24},{16,0},{24,8},{32,48},{40,56},{48,32},{56,40},{64,80... | collective-permute-start | bytes 110600 | tf_op jit(solution)/shard_map/ppermute | solution.py:485
  40.6 1.9 %multiply_sine_fusion = (f32[640,10]{1,0:T(8,128)}, f32[640,10]{1,0:T(8,128)}) fusion(f32[640,10]{1,0:T(8,128)S(1)} %copy.16), kind=kLoop, calls=%fused_computation.11 | loop fusion | flops 6400 | bytes 76800 | tf_op jit(solution)/shard_map/sin | solution.py:191
  43.3 3.3 %collective-permute-start.4 = (bf16[72,128]{1,0:T(8,128)(2,1)S(1)}, bf16[72,128]{1,0:T(8,128)(2,1)S(1)}, u32[]{:S(2)}, u32[]{:S(2)}) collective-permute-start(bf16[72,128]{1,0:T(8,128)(2,1)S(1)} %select_convert_fusion.4), channel_id=1, source_target_pairs={{0,64},{8,72},{16,80},{24,88},{32,96},{40,104},{48,112},{56,120},{... | collective-permute-start | bytes 55304 | tf_op jit(solution)/shard_map/ppermute | solution.py:485
  46.6 1.4 sine_multiply_fusion
  49.0 1.0 copy-done.2
  50.0 1.8 waves.1.table_ref
  51.8 10.1 %all-to-all-done = bf16[8,160,896]{2,1,0:T(8,128)(2,1)} async-done(((bf16[8,160,896]{2,1,0:T(8,128)(2,1)}), bf16[8,160,896]{2,1,0:T(8,128)(2,1)}, u32[]{:S(2)}, u32[]{:S(2)}) %all-to-all-start) | async-done | bytes 2293792 | tf_op jit(solution)/shard_map/all_to_all | solution.py:505
  62.0 6.9 %forward.1 = bf16[128,72,128]{2,1,0:T(8,128)(2,1)S(1)} custom-call(bf16[1280,896]{1,0:T(8,128)(2,1)} %bitcast.1.x_ref, bf16[1280,1280]{1,0:T(8,128)(2,1)S(1)} %waves.1.table_ref, f32[72,128]{1,0:T(8,128)S(1)} %convert_add_fusion.4.grad_ref), custom_call_target="tpu_custom_call" | custom-call | tf_op jit(solution)/shard_map/forward/pallas_call | solution.py:293
  68.9 1.4 copy-done
  70.3 8.4 %all-to-all-start.1 = ((bf16[128,72,128]{2,1,0:T(8,128)(2,1)}), bf16[128,72,128]{2,1,0:T(8,128)(2,1)}, u32[]{:S(2)}, u32[]{:S(2)}) async-start(bf16[128,72,128]{2,1,0:T(8,128)(2,1)} %copy-done), calls=%async_computation.1 | async-start | bytes 4718592 | tf_op jit(solution)/shard_map/all_to_all | solution.py:505
  79.2 18.7 %copy.17 = bf16[88,88,640]{1,0,2:T(8,128)(2,1)} copy(bf16[88,88,640]{2,1,0:T(8,128)(2,1)} %param.14) | data formatting | bytes 19824640 | tf_op jit(solution)/shard_map/optimization_barrier | solution.py:510
  98.0 9.7 %legendre.1 = (bf16[5,640,640]{2,1,0:T(8,128)(2,1)}, bf16[5,640,640]{2,1,0:T(8,128)(2,1)}) custom-call(s32[5]{0:T(128)} %dynamic_slice.3.m_ref, bf16[5,320,640]{2,1,0:T(8,128)(2,1)} %leg_ref), custom_call_target="tpu_custom_call" | custom-call | tf_op jit(solution)/shard_map/legendre/pallas_call | solution.py:222
  107.7 3.8 %all-to-all-done.1.in_hbm = bf16[128,72,128]{2,1,0:T(8,128)(2,1)} async-done(((bf16[128,72,128]{2,1,0:T(8,128)(2,1)}), bf16[128,72,128]{2,1,0:T(8,128)(2,1)}, u32[]{:S(2)}, u32[]{:S(2)}) %all-to-all-start.1) | async-done | bytes 2359328 | tf_op jit(solution)/shard_map/all_to_all | solution.py:505
  111.5 23.4 %spectral.1 = bf16[128,88,128]{2,1,0:T(8,128)(2,1)} custom-call(s32[5]{0:T(128)} %dynamic_slice.3.m_ref, bf16[128,72,128]{2,1,0:T(8,128)(2,1)} %all-to-all-done.1.in_hbm, bf16[5,640,640]{2,1,0:T(8,128)(2,1)} %get-tuple-element.27.at_hbm, bf16[640,88,88]{2,1,0:T(8,128)(2,1)} %bitcast.6, bf16[5,640,640]{2,1,0:T(8,128)(2,1)} %get-tuple-element.29.as_hbm), custom_call_target="tpu_custom_call" | custom-call | tf_op jit(solution)/shard_map/spectral/pallas_call | solution.py:403
  134.9 44.8 %all_to_all.15.in_hbm = bf16[128,88,128]{2,1,0:T(8,128)(2,1)S(1)} all-to-all(bf16[128,88,128]{2,1,0:T(8,128)(2,1)} %spectral.1), channel_id=1, replica_groups=mesh['lat'=16,'lev'=8] {'lat','lev'}, dimensions={0} | all-to-all | bytes 5767168 | tf_op jit(solution)/shard_map/all_to_all | solution.py:505
  179.7 6.8 %inverse.1 = (f32[5,176,1280]{2,1,0:T(8,128)}, f32[176,384]{1,0:T(8,128)}, f32[384,384]{1,0:T(8,128)}, f32[176,384]{1,0:T(8,128)}) custom-call(bf16[128,88,128]{2,1,0:T(8,128)(2,1)S(1)} %all_to_all.15.in_hbm, bf16[1280,1280]{1,0:T(8,128)(2,1)S(1)} %waves.1.table_ref), custom_call_target="tpu_custom_call" | custom-call | tf_op jit(solution)/shard_map/inverse/pallas_call | solution.py:460
  (24 shorter events, 3.2 us)
Async XLA Ops:
  22.5 1.7 collective-permute-start
  25.6 7.0 %copy-start.3 = (s32[640]{0:T(1024)S(1)}, s32[640]{0:T(1024)}, u32[]{:S(2)}) copy-start(s32[640]{0:T(1024)} %param.15) | copy-start | bytes 7684
  25.6 7.3 %collective-permute-start.1 = (bf16[576,128]{1,0:T(8,128)(2,1)S(1)}, bf16[576,128]{1,0:T(8,128)(2,1)S(1)}, u32[]{:S(2)}, u32[]{:S(2)}) collective-permute-start(bf16[576,128]{1,0:T(8,128)(2,1)S(1)} %select_convert_fusion.1), channel_id=1, source_target_pairs={{0,8},{8,0},{16,24},{24,16},{32,40},{40,32},{48,56},{56,48},{64,72... | collective-permute-start | bytes 442376 | tf_op jit(solution)/shard_map/ppermute | solution.py:485
  27.3 34.7 %all-to-all-start = ((bf16[8,160,896]{2,1,0:T(8,128)(2,1)}), bf16[8,160,896]{2,1,0:T(8,128)(2,1)}, u32[]{:S(2)}, u32[]{:S(2)}) async-start(bf16[8,160,896]{2,1,0:T(8,128)(2,1)} %bitcast), calls=%async_computation | async-start | bytes 4587520 | tf_op jit(solution)/shard_map/all_to_all | solution.py:505
  32.9 4.8 %collective-permute-start.2 = (bf16[288,128]{1,0:T(8,128)(2,1)S(1)}, bf16[288,128]{1,0:T(8,128)(2,1)S(1)}, u32[]{:S(2)}, u32[]{:S(2)}) collective-permute-start(bf16[288,128]{1,0:T(8,128)(2,1)S(1)} %select_convert_fusion.2), channel_id=1, source_target_pairs={{0,32},{8,40},{16,48},{24,56},{32,0},{40,8},{48,16},{56,24},{64,96... | collective-permute-start | bytes 221192 | tf_op jit(solution)/shard_map/ppermute | solution.py:485
  37.7 5.5 %collective-permute-start.3 = (bf16[144,128]{1,0:T(8,128)(2,1)S(1)}, bf16[144,128]{1,0:T(8,128)(2,1)S(1)}, u32[]{:S(2)}, u32[]{:S(2)}) collective-permute-start(bf16[144,128]{1,0:T(8,128)(2,1)S(1)} %select_convert_fusion.3), channel_id=1, source_target_pairs={{0,16},{8,24},{16,0},{24,8},{32,48},{40,56},{48,32},{56,40},{64,80... | collective-permute-start | bytes 110600 | tf_op jit(solution)/shard_map/ppermute | solution.py:485
  43.3 8.5 %collective-permute-start.4 = (bf16[72,128]{1,0:T(8,128)(2,1)S(1)}, bf16[72,128]{1,0:T(8,128)(2,1)S(1)}, u32[]{:S(2)}, u32[]{:S(2)}) collective-permute-start(bf16[72,128]{1,0:T(8,128)(2,1)S(1)} %select_convert_fusion.4), channel_id=1, source_target_pairs={{0,64},{8,72},{16,80},{24,88},{32,96},{40,104},{48,112},{56,120},{... | collective-permute-start | bytes 55304 | tf_op jit(solution)/shard_map/ppermute | solution.py:485
  48.0 1.0 copy-start.1
  49.0 1.0 copy-start.2
  68.9 1.4 copy-start
  70.3 41.2 %all-to-all-start.1 = ((bf16[128,72,128]{2,1,0:T(8,128)(2,1)}), bf16[128,72,128]{2,1,0:T(8,128)(2,1)}, u32[]{:S(2)}, u32[]{:S(2)}) async-start(bf16[128,72,128]{2,1,0:T(8,128)(2,1)} %copy-done), calls=%async_computation.1 | async-start | bytes 4718592 | tf_op jit(solution)/shard_map/all_to_all | solution.py:505
